TPU v7x, 128 devices: a whole 4x4x4 slice. The times are simulated.
128 devices in a mesh: rep: 64 (over z, y, x), data: 2 (over core).
Axes of the slice: x: 4, y: 4, z: 4, core: 2. Of those that a mesh axis runs over, the one named last changes fastest.
Arguments:
- act_in: bfloat16 [131072, 1024], P(('rep', 'data'))
- grad_out: bfloat16 [131072, 1024], P(('rep', 'data'))
- w_one: bfloat16 [1024, 3072], replicated
- w_two: bfloat16 [3072, 1024], replicated
- w_three: bfloat16 [1024, 3072], replicated
- w_four: bfloat16 [3072, 1024], replicated
- master_one: float32 [1024, 3072], P('data')
- master_two: float32 [3072, 1024], P('data')
- master_three: float32 [1024, 3072], P('data')
- master_four: float32 [3072, 1024], P('data')
- mom_one: float32 [1024, 3072], P('data')
- mom_two: float32 [3072, 1024], P('data')
- mom_three: float32 [1024, 3072], P('data')
- mom_four: float32 [3072, 1024], P('data')
- vel_one: float32 [1024, 3072], P('data')
- vel_two: float32 [3072, 1024], P('data')
- vel_three: float32 [1024, 3072], P('data')
- vel_four: float32 [3072, 1024], P('data')
- clip_norm: float32 [], replicated
Outputs:
- output 1: bfloat16 [1024, 3072], replicated
- output 2: bfloat16 [3072, 1024], replicated
- output 3: bfloat16 [1024, 3072], replicated
- output 4: bfloat16 [3072, 1024], replicated
- output 5: float32 [1024, 3072], P('data')
- output 6: float32 [3072, 1024], P('data')
- output 7: float32 [1024, 3072], P('data')
- output 8: float32 [3072, 1024], P('data')
- output 9: float32 [1024, 3072], P('data')
- output 10: float32 [3072, 1024], P('data')
- output 11: float32 [1024, 3072], P('data')
- output 12: float32 [3072, 1024], P('data')
- output 13: float32 [1024, 3072], P('data')
- output 14: float32 [3072, 1024], P('data')
- output 15: float32 [1024, 3072], P('data')
- output 16: float32 [3072, 1024], P('data')
- output 17: float32 [], replicated
All inputs are finite; a program needn't handle non-finite values.
Results may differ from a plain program's by a relative error of at most 0.00368133.
Values are sent between devices in bfloat16 or wider.
A program may use at most 1 GiB of HBM per device.

v0:
```python
import jax
import jax.numpy as jnp
from jax import lax
from jax.sharding import PartitionSpec as P

TRAIN_STEP = 10
BETA_ONE = 0.9
BETA_TWO = 0.95
ADAM_EPS = 1e-8
NORM_EPS = 1e-6
LEARN_RATE = 0.003
CONT_ROWS = (((0,), (0,)), ((), ()))
CONT_COLS = (((1,), (1,)), ((), ()))


def gelu_fn(values):
    return jax.nn.gelu(values, approximate=True)


def local_grads(act_in, grad_out, w_one, w_two, w_three, w_four):
    h_one = jnp.dot(act_in, w_one, preferred_element_type=jnp.float32).astype(jnp.bfloat16)
    a_one_f, back_one = jax.vjp(gelu_fn, h_one.astype(jnp.float32))
    a_one = a_one_f.astype(jnp.bfloat16)
    y_one = jnp.dot(a_one, w_two, preferred_element_type=jnp.float32).astype(jnp.bfloat16)
    h_two = jnp.dot(y_one, w_three, preferred_element_type=jnp.float32).astype(jnp.bfloat16)
    a_two_f, back_two = jax.vjp(gelu_fn, h_two.astype(jnp.float32))
    a_two = a_two_f.astype(jnp.bfloat16)
    g_four = lax.dot_general(a_two, grad_out, CONT_ROWS, preferred_element_type=jnp.float32)
    da_two = lax.dot_general(grad_out, w_four, CONT_COLS, preferred_element_type=jnp.float32).astype(jnp.bfloat16)
    dh_two = back_two(da_two.astype(jnp.float32))[0].astype(jnp.bfloat16)
    g_three = lax.dot_general(y_one, dh_two, CONT_ROWS, preferred_element_type=jnp.float32)
    dy_one = lax.dot_general(dh_two, w_three, CONT_COLS, preferred_element_type=jnp.float32).astype(jnp.bfloat16)
    g_two = lax.dot_general(a_one, dy_one, CONT_ROWS, preferred_element_type=jnp.float32)
    da_one = lax.dot_general(dy_one, w_two, CONT_COLS, preferred_element_type=jnp.float32).astype(jnp.bfloat16)
    dh_one = back_one(da_one.astype(jnp.float32))[0].astype(jnp.bfloat16)
    g_one = lax.dot_general(act_in, dh_one, CONT_ROWS, preferred_element_type=jnp.float32)
    return g_one, g_two, g_three, g_four


def adam_update(gradient, master, mom_in, vel_in, clip_scale):
    scaled = clip_scale * gradient
    mom_new = BETA_ONE * mom_in + (1.0 - BETA_ONE) * scaled
    vel_new = BETA_TWO * vel_in + (1.0 - BETA_TWO) * jnp.square(scaled)
    corr_one = 1.0 - BETA_ONE ** TRAIN_STEP
    corr_two = 1.0 - BETA_TWO ** TRAIN_STEP
    master_new = master - LEARN_RATE * (mom_new / corr_one) / (jnp.sqrt(vel_new / corr_two) + ADAM_EPS)
    return master_new, mom_new, vel_new


def solution(mesh):
    dev_count = mesh.shape['rep'] * mesh.shape['data']
    row_spec = P(('rep', 'data'), None)
    shard_spec = P('data', None)
    full_spec = P()

    def per_device(act_in, grad_out, w_one, w_two, w_three, w_four, master_one, master_two, master_three, master_four, mom_one, mom_two, mom_three, mom_four, vel_one, vel_two, vel_three, vel_four, clip_norm):
        local_list = local_grads(act_in, grad_out, w_one, w_two, w_three, w_four)
        reduced = {}
        for mat_idx in (3, 2, 1, 0):
            row_part = lax.psum_scatter(local_list[mat_idx], 'data', scatter_dimension=0, tiled=True)
            reduced[mat_idx] = lax.psum(row_part, 'rep') / dev_count
        sq_local = sum(jnp.sum(jnp.square(reduced[mat_idx])) for mat_idx in range(4))
        grad_norm = jnp.sqrt(lax.psum(sq_local, 'data'))
        clip_scale = jnp.minimum(1.0, clip_norm / (grad_norm + NORM_EPS))
        master_list = (master_one, master_two, master_three, master_four)
        mom_list = (mom_one, mom_two, mom_three, mom_four)
        vel_list = (vel_one, vel_two, vel_three, vel_four)
        upd_list = [adam_update(reduced[mat_idx], master_list[mat_idx], mom_list[mat_idx], vel_list[mat_idx], clip_scale) for mat_idx in range(4)]
        new_weights = tuple(lax.all_gather(upd_set[0].astype(jnp.bfloat16), 'data', axis=0, tiled=True) for upd_set in upd_list)
        return new_weights + tuple(upd_set[0] for upd_set in upd_list) + tuple(upd_set[1] for upd_set in upd_list) + tuple(upd_set[2] for upd_set in upd_list) + (grad_norm,)

    in_specs = (row_spec, row_spec, full_spec, full_spec, full_spec, full_spec) + (shard_spec,) * 12 + (full_spec,)
    out_specs = (full_spec,) * 4 + (shard_spec,) * 12 + (full_spec,)
    return jax.shard_map(per_device, mesh=mesh, in_specs=in_specs, out_specs=out_specs, check_vma=False)
```

profile of v0, /device:TPU:1, one launch (start us, length us, event | category | flops | bytes accessed | tf_op | source)
XLA Modules:
  0.0 629.5 jit_solution(944912987820851104)
XLA Ops:
  7.2 0.0 reduce-scatter.9.cloned.1.call-start
  7.3 11.2 %convolution_convert_fusion.1 = bf16[1024,3072]{1,0:T(8,128)(2,1)} fusion(bf16[1024,1024]{1,0:T(8,128)(2,1)} %param.19, bf16[1024,3072]{1,0:T(8,128)(2,1)} %param.21), kind=kOutput, calls=%fused_computation.57 | convolution fusion | flops 6445596672 | bytes 14680064 | tf_op jit(solution)/shard_map/dot_general | solution.py:21
  18.5 10.4 %convolution_convert_fusion.3 = bf16[1024,1024]{1,0:T(8,128)(2,1)S(1)} fusion(bf16[3072,1024]{1,0:T(8,128)(2,1)S(1)} %copy-done.6, bf16[1024,3072]{1,0:T(8,128)(2,1)} %convolution_convert_fusion.1), kind=kOutput, calls=%fused_computation.60 | convolution fusion | flops 6474956800 | bytes 14680064 | tf_op jit(solution)/shard_map/dot_general | solution.py:24
  28.9 8.6 %convolution_convert_fusion = bf16[1024,3072]{1,0:T(8,128)(2,1)} fusion(bf16[1024,1024]{1,0:T(8,128)(2,1)S(1)} %convolution_convert_fusion.3, bf16[1024,3072]{1,0:T(8,128)(2,1)S(1)} %copy-done.5), kind=kOutput, calls=%fused_computation.56 | convolution fusion | flops 6445596672 | bytes 14680064 | tf_op jit(solution)/shard_map/dot_general | solution.py:25
  37.5 15.1 %fusion.4 = bf16[1024,3072]{1,0:T(8,128)(2,1)S(1)} fusion(bf16[1024,3072]{1,0:T(8,128)(2,1)} %convolution_convert_fusion, bf16[1024,1024]{1,0:T(8,128)(2,1)S(1)} %copy-done, bf16[3072,1024]{1,0:T(8,128)(2,1)S(1)} %bitcast.19), kind=kOutput, calls=%fused_computation.16 | convolution fusion | flops 6514802688 | bytes 20971520 | tf_op jit(solution)/shard_map/dot_general | solution.py:29
  52.6 2.7 copy-done.8
  55.3 9.8 %fusion.48 = f32[1024,3072]{0,1:T(8,128)} fusion(bf16[1024,1024]{1,0:T(8,128)(2,1)S(1)} %convolution_convert_fusion.3, bf16[1024,3072]{1,0:T(8,128)(2,1)S(1)} %fusion.4), kind=kOutput, calls=%fused_computation.76 | convolution fusion | flops 6442450944 | bytes 20971520 | tf_op jit(solution)/shard_map/dot_general | solution.py:31
  65.1 0.0 reduce-scatter.11.cloned.1.call-start
  65.2 13.9 %fusion.22 = f32[3072,1024]{1,0:T(8,128)} fusion(bf16[1024,1024]{1,0:T(8,128)(2,1)S(1)} %copy-done, bf16[1024,3072]{1,0:T(8,128)(2,1)} %convolution_convert_fusion), kind=kOutput, calls=%fused_computation.35 | convolution fusion | flops 6473908224 | bytes 20971520 | tf_op jit(solution)/shard_map/dot_general | solution.py:28
  79.0 0.0 reduce-scatter.7.cloned.1.call-start
  79.1 10.7 %convolution_convert_fusion.2 = bf16[1024,1024]{1,0:T(8,128)(2,1)S(1)} fusion(bf16[1024,3072]{1,0:T(8,128)(2,1)} %copy-done.8, bf16[1024,3072]{1,0:T(8,128)(2,1)} %param.23), kind=kOutput, calls=%fused_computation.59 | convolution fusion | flops 6443499520 | bytes 14680064 | tf_op jit(solution)/shard_map/dot_general | solution.py:32
  89.8 14.7 %fusion.41 = f32[3072,1024]{1,0:T(8,128)} fusion(bf16[1024,1024]{1,0:T(8,128)(2,1)S(1)} %convolution_convert_fusion.2, bf16[1024,3072]{1,0:T(8,128)(2,1)} %convolution_convert_fusion.1), kind=kOutput, calls=%fused_computation.71 | convolution fusion | flops 6473908224 | bytes 20971520 | tf_op jit(solution)/shard_map/dot_general | solution.py:33
  104.6 0.0 reduce-scatter.5.cloned.1.call-start
  104.6 1.5 copy-done.7
  106.1 24.3 %convolution_bitcast_fusion = f32[1024,3072]{0,1:T(8,128)} fusion(bf16[1024,1024]{1,0:T(8,128)(2,1)S(1)} %copy-done.7, bf16[1024,3072]{1,0:T(8,128)(2,1)} %convolution_convert_fusion.1, bf16[1024,1024]{1,0:T(8,128)(2,1)} %copy-done.9, bf16[3072,1024]{1,0:T(8,128)(2,1)} %param.22), kind=kOutput, calls=%fused_computation.34 | convolution fusion | flops 12957253632 | bytes 29360128 | tf_op jit(solution)/shard_map/dot_general | solution.py:36
  130.4 0.0 all-reduce.3.cloned.1.call-start
  130.5 0.0 reduce-scatter.9.cloned.1.call-done
  130.5 9.9 %reduce-scatter.7.cloned.1.call-done = f32[1536,1024]{1,0:T(8,128)} async-done(((f32[3072,1024]{1,0:T(8,128)}), f32[1536,1024]{1,0:T(8,128)}) %reduce-scatter.7.cloned.1.call-update) | async-done | bytes 6291472 | tf_op jit(solution)/shard_map/reduce_scatter | solution.py:60
  140.4 24.9 %reduce-scatter.5.cloned.1.call-done = f32[512,3072]{0,1:T(8,128)} async-done(((f32[1024,3072]{0,1:T(8,128)}), f32[512,3072]{0,1:T(8,128)}) %reduce-scatter.5.cloned.1.call-update) | async-done | bytes 6291472 | tf_op jit(solution)/shard_map/reduce_scatter | solution.py:60
  165.3 0.0 all-gather.9.cloned.1.call-start
  166.0 6.6 %copy.42 = f32[512,3072]{0,1:T(8,128)} copy(f32[512,3072]{1,0:T(8,128)} %param.27) | data formatting | bytes 12582912 | tf_op args[8]
  172.6 6.6 %copy.40 = f32[512,3072]{0,1:T(8,128)} copy(f32[512,3072]{1,0:T(8,128)} %param.31) | data formatting | bytes 12582912 | tf_op args[12]
  179.1 260.3 %all-reduce.3.cloned.1.call-done = (f32[512,3072]{0,1:T(8,128)}, f32[1536,1024]{1,0:T(8,128)}, f32[512,3072]{0,1:T(8,128)}, f32[1536,1024]{1,0:T(8,128)}) async-done(((f32[512,3072]{0,1:T(8,128)}, f32[1536,1024]{1,0:T(8,128)}, f32[512,3072]{0,1:T(8,128)}, f32[1536,1024]{1,0:T(8,128)}), (f32[512,3072]{0,1:T(8,128)}, f32[1536,1024]{1,0:T(8,128)}, f32[512,3072]{0,1:T(8,128)}, ...) | async-done | bytes 25165840 | tf_op jit(solution)/shard_map/psum | solution.py:61
  439.4 7.1 %multiply_reduce_fusion.1 = (f32[]{:T(128)}, f32[]{:T(128)}) fusion(f32[512,3072]{0,1:T(8,128)} %get-tuple-element.36, f32[512,3072]{0,1:T(8,128)} %get-tuple-element.34), kind=kLoop, calls=%fused_computation.49 | loop fusion | flops 9437182 | bytes 12582920 | tf_op jit(solution)/shard_map/reduce_sum | solution.py:62
  446.5 1.1 copy-done.3
  447.6 2.2 multiply_reduce_fusion
  452.4 6.6 %copy.41 = f32[512,3072]{0,1:T(8,128)} copy(f32[512,3072]{1,0:T(8,128)} %param.35) | data formatting | bytes 12582912 | tf_op args[16]
  459.0 5.2 psum.39
  464.9 18.1 %fusion.45 = (bf16[512,3072]{0,1:T(8,128)(2,1)}, f32[512,3072]{0,1:T(8,128)}, f32[512,3072]{0,1:T(8,128)}, f32[512,3072]{0,1:T(8,128)}) fusion(f32[512,3072]{0,1:T(8,128)} %copy.42, f32[512,3072]{0,1:T(8,128)} %get-tuple-element.36, f32[]{:T(128)S(6)} %mul.194, f32[512,3072]{0,1:T(8,128)} %copy.40, f32[512,3072]{0,1:T(8,128)} %copy.41), kind=kLoop, calls=%fused_computation.73 | loop fusion | flops 22020096 | bytes 47185924 | tf_op jit(solution)/shard_map/convert_element_type | solution.py:69
  483.0 0.0 all-gather.5.cloned.1.call-start
  483.1 6.6 %copy.39 = f32[512,3072]{0,1:T(8,128)} copy(f32[512,3072]{1,0:T(8,128)} %param.25) | data formatting | bytes 12582912 | tf_op args[6]
  489.6 6.6 %copy.36 = f32[512,3072]{0,1:T(8,128)} copy(f32[512,3072]{1,0:T(8,128)} %param.29) | data formatting | bytes 12582912 | tf_op args[10]
  496.2 6.6 %copy.38 = f32[512,3072]{0,1:T(8,128)} copy(f32[512,3072]{1,0:T(8,128)} %param.33) | data formatting | bytes 12582912 | tf_op args[14]
  502.7 17.9 %fusion.47 = (bf16[512,3072]{0,1:T(8,128)(2,1)}, f32[512,3072]{0,1:T(8,128)}, f32[512,3072]{0,1:T(8,128)}, f32[512,3072]{0,1:T(8,128)}) fusion(f32[512,3072]{0,1:T(8,128)} %copy.39, f32[512,3072]{0,1:T(8,128)} %get-tuple-element.34, f32[]{:T(128)S(6)} %mul.194, f32[512,3072]{0,1:T(8,128)} %copy.36, f32[512,3072]{0,1:T(8,128)} %copy.38), kind=kLoop, calls=%fused_computation.75 | loop fusion | flops 22020096 | bytes 47185924 | tf_op jit(solution)/shard_map/convert_element_type | solution.py:69
  520.6 0.0 all-gather.11.cloned.1.call-start
  520.7 17.3 %fusion.44 = (bf16[1536,1024]{1,0:T(8,128)(2,1)}, f32[1536,1024]{1,0:T(8,128)}, f32[1536,1024]{1,0:T(8,128)}, f32[1536,1024]{1,0:T(8,128)}) fusion(f32[1536,1024]{1,0:T(8,128)} %param.28, f32[1536,1024]{1,0:T(8,128)} %get-tuple-element.37, f32[]{:T(128)S(6)} %mul.194, f32[1536,1024]{1,0:T(8,128)} %param.32, f32[1536,1024]{1,0:T(8,128)} %param.36), kind=kLoop, calls=%fused_computation.72 | loop fusion | flops 22020096 | bytes 47185924 | tf_op jit(solution)/shard_map/convert_element_type | solution.py:69
  538.0 0.0 all-gather.7.cloned.1.call-start
  538.0 17.6 %fusion.46 = (bf16[1536,1024]{1,0:T(8,128)(2,1)}, f32[1536,1024]{1,0:T(8,128)}, f32[1536,1024]{1,0:T(8,128)}, f32[1536,1024]{1,0:T(8,128)}) fusion(f32[1536,1024]{1,0:T(8,128)} %param.26, f32[1536,1024]{1,0:T(8,128)} %get-tuple-element.35, f32[]{:T(128)S(6)} %mul.194, f32[1536,1024]{1,0:T(8,128)} %param.30, f32[1536,1024]{1,0:T(8,128)} %param.34), kind=kLoop, calls=%fused_computation.74 | loop fusion | flops 22020096 | bytes 47185924 | tf_op jit(solution)/shard_map/convert_element_type | solution.py:69
  555.6 6.6 %copy.46 = f32[512,3072]{1,0:T(8,128)} copy(f32[512,3072]{0,1:T(8,128)} %get-tuple-element.43) | data formatting | bytes 12582912
  562.2 6.6 %copy.48 = f32[512,3072]{1,0:T(8,128)} copy(f32[512,3072]{0,1:T(8,128)} %get-tuple-element.44) | data formatting | bytes 12582912
  568.8 6.6 %copy.50 = f32[512,3072]{1,0:T(8,128)} copy(f32[512,3072]{0,1:T(8,128)} %get-tuple-element.45) | data formatting | bytes 12582912
  575.3 6.6 %copy.45 = f32[512,3072]{1,0:T(8,128)} copy(f32[512,3072]{0,1:T(8,128)} %get-tuple-element.51) | data formatting | bytes 12582912
  581.9 6.6 %copy.47 = f32[512,3072]{1,0:T(8,128)} copy(f32[512,3072]{0,1:T(8,128)} %get-tuple-element.52) | data formatting | bytes 12582912
  588.5 6.6 %copy.49 = f32[512,3072]{1,0:T(8,128)} copy(f32[512,3072]{0,1:T(8,128)} %get-tuple-element.53) | data formatting | bytes 12582912
  595.0 8.6 %copy.44 = bf16[1024,3072]{1,0:T(8,128)(2,1)} copy(bf16[1024,3072]{0,1:T(8,128)(2,1)} %all-gather.9.cloned.1.call-done) | data formatting | bytes 12582912
  603.6 8.6 %copy.43 = bf16[1024,3072]{1,0:T(8,128)(2,1)} copy(bf16[1024,3072]{0,1:T(8,128)(2,1)} %all-gather.5.cloned.1.call-done) | data formatting | bytes 12582912
  612.3 6.4 %copy.59 = bf16[3072,1024]{1,0:T(8,128)(2,1)} copy(bf16[3072,1024]{1,0:T(8,128)(2,1)} %all-gather.7.cloned.1.call-done) | data formatting | bytes 12582912
  618.7 2.7 copy.60
  (36 shorter events, 0.2 us)
Async XLA Ops:
  7.2 30.3 %copy-start = (bf16[1024,1024]{1,0:T(8,128)(2,1)S(1)}, bf16[1024,1024]{1,0:T(8,128)(2,1)}, u32[]{:S(2)}) copy-start(bf16[1024,1024]{1,0:T(8,128)(2,1)} %param.20) | copy-start | bytes 6291460
  7.2 123.3 %reduce-scatter.9.cloned.1.call-start = ((), (), s32[]{:S(2)}) async-start(), calls=%async_computation.6 | async-start | bytes 18874368 | tf_op jit(solution)/shard_map/reduce_scatter | solution.py:60
  7.3 11.2 %copy-start.6 = (bf16[3072,1024]{1,0:T(8,128)(2,1)S(1)}, bf16[3072,1024]{1,0:T(8,128)(2,1)}, u32[]{:S(2)}) copy-start(bf16[3072,1024]{1,0:T(8,128)(2,1)} %param.22) | copy-start | bytes 18874372
  18.5 10.4 %copy-start.5 = (bf16[1024,3072]{1,0:T(8,128)(2,1)S(1)}, bf16[1024,3072]{1,0:T(8,128)(2,1)}, u32[]{:S(2)}) copy-start(bf16[1024,3072]{1,0:T(8,128)(2,1)} %param.23) | copy-start | bytes 18874372
  18.5 19.0 %slice-start = ((s8[6291456]{0:T(1024)(128)(4,1)}), s8[4194304]{0:T(1024)(128)(4,1)S(1)}, s32[]{:S(2)}) async-start(s8[6291456]{0:T(1024)(128)(4,1)} %bitcast.18), calls=%async_computation.13 | async-start | bytes 8388608
  28.9 8.6 %slice-start.1 = ((s8[6291456]{0:T(1024)(128)(4,1)}), s8[2097152]{0:T(1024)(128)(4,1)S(1)}, s32[]{:S(2)}) async-start(s8[6291456]{0:T(1024)(128)(4,1)} %bitcast.18), calls=%async_computation.14 | async-start | bytes 4194304
  52.6 2.7 copy-start.8
  65.1 65.4 %reduce-scatter.11.cloned.1.call-start = ((), (), s32[]{:S(2)}) async-start(), calls=%async_computation.7 | async-start | bytes 18874368 | tf_op jit(solution)/shard_map/reduce_scatter | solution.py:60
  79.0 61.3 %reduce-scatter.7.cloned.1.call-start = ((), (), s32[]{:S(2)}) async-start(), calls=%async_computation.5 | async-start | bytes 18874368 | tf_op jit(solution)/shard_map/reduce_scatter | solution.py:60
  89.8 14.7 %copy-start.9 = (bf16[1024,1024]{1,0:T(8,128)(2,1)}, bf16[1024,1024]{1,0:T(8,128)(2,1)S(1)}, u32[]{:S(2)}) copy-start(bf16[1024,1024]{1,0:T(8,128)(2,1)S(1)} %convolution_convert_fusion.2) | copy-start | bytes 6291460
  104.5 1.6 copy-start.7
  104.6 60.7 %reduce-scatter.5.cloned.1.call-start = ((), (), s32[]{:S(2)}) async-start(), calls=%async_computation.4 | async-start | bytes 18874368 | tf_op jit(solution)/shard_map/reduce_scatter | solution.py:60
  130.4 309.0 %all-reduce.3.cloned.1.call-start = ((), (), s32[]{:S(2)}) async-start(), calls=%async_computation.12 | async-start | bytes 50331648 | tf_op jit(solution)/shard_map/psum | solution.py:61
  165.3 429.7 %all-gather.9.cloned.1.call-start = ((), (), s32[]{:S(2)}) async-start(), calls=%async_computation.10 | async-start | bytes 9437184 | tf_op jit(solution)/shard_map/all_gather | solution.py:69
  439.4 7.1 %copy-start.2 = (f32[1536,1024]{1,0:T(8,128)S(1)}, f32[1536,1024]{1,0:T(8,128)}, u32[]{:S(2)}) copy-start(f32[1536,1024]{1,0:T(8,128)} %get-tuple-element.35) | copy-start | bytes 18874372
  439.4 8.2 %copy-start.3 = (f32[1536,1024]{1,0:T(8,128)S(1)}, f32[1536,1024]{1,0:T(8,128)}, u32[]{:S(2)}) copy-start(f32[1536,1024]{1,0:T(8,128)} %get-tuple-element.37) | copy-start | bytes 18874372
  483.0 120.6 %all-gather.5.cloned.1.call-start = ((), (), s32[]{:S(2)}) async-start(), calls=%async_computation.8 | async-start | bytes 9437184 | tf_op jit(solution)/shard_map/all_gather | solution.py:69
  520.6 91.6 %all-gather.11.cloned.1.call-start = ((), (), s32[]{:S(2)}) async-start(), calls=%async_computation.11 | async-start | bytes 9437184 | tf_op jit(solution)/shard_map/all_gather | solution.py:69
  538.0 74.3 %all-gather.7.cloned.1.call-start = ((), (), s32[]{:S(2)}) async-start(), calls=%async_computation.9 | async-start | bytes 9437184 | tf_op jit(solution)/shard_map/all_gather | solution.py:69
  612.3 6.4 %copy-start.4 = (bf16[3072,1024]{1,0:T(8,128)(2,1)S(1)}, bf16[3072,1024]{1,0:T(8,128)(2,1)}, u32[]{:S(2)}) copy-start(bf16[3072,1024]{1,0:T(8,128)(2,1)} %all-gather.11.cloned.1.call-done) | copy-start | bytes 18874372
  612.3 9.1 %copy-start.1 = (bf16[1024,1024]{1,0:T(8,128)(2,1)S(1)}, bf16[1024,1024]{1,0:T(8,128)(2,1)}, u32[]{:S(2)}) copy-start(bf16[1024,1024]{1,0:T(8,128)(2,1)} %param.20) | copy-start | bytes 6291460
Sparse Core Ops, SparseCore 0:
  65.2 24.9 reduce-scatter.8
  92.6 22.6 reduce-scatter.10
  117.7 22.5 reduce-scatter.6
  142.6 22.6 reduce-scatter.4
  171.4 267.9 all-reduce.2
  483.1 17.8 all-gather.8
  520.7 17.8 all-gather.4
  540.3 21.4 all-gather.10
  563.4 21.4 all-gather.6
where the time goes:
time: 638 us; the launch traced here: 629 us
  waiting for transfers between devices  295 us (46%)
  matrix products  119 us (19%)
  local copies, waits for them, and re-layouts  110 us (17%)
  other arithmetic  80.1 us (13%)
  between operations  19.5 us (3%)
    psum x1, waiting for transfers between devices, per_device(): reduced[mat_idx] = lax.psum(row_part, 'rep') / dev_count  260 us
    unnamed x40, local copies, waits for them, and re-layouts  110 us
    convert_element_type x4, other arithmetic, per_device(): upd_set[0].astype(jnp.bfloat16)  70.8 us
    reduce_scatter x4, waiting for transfers between devices, per_device(): lax.psum_scatter(local_list[mat_idx], 'data', scatter_dimension=0, tiled=...  34.8 us
    dot_general x1, matrix products, local_grads(): lax.dot_general(act_in, dh_one, CONT_ROWS, preferred_element_type=jnp.flo...  24.3 us
    dot_general x1, matrix products, local_grads(): lax.dot_general(grad_out, w_four, CONT_COLS, preferred_element_type=jnp.f...  15.1 us
    dot_general x1, matrix products, local_grads(): lax.dot_general(a_one, dy_one, CONT_ROWS, preferred_element_type=jnp.floa...  14.7 us
    dot_general x1, matrix products, local_grads(): lax.dot_general(a_two, grad_out, CONT_ROWS, preferred_element_type=jnp.fl...  13.9 us
  transfers between devices with their start and end apart: 9, of which 3 were waited for; matrix products, arithmetic and copies ran while one was open for 33% of the time, Pallas kernels for 0%

commit v1 on v0

v1 whole, which is shorter than its diff:
```python
import jax
import jax.numpy as jnp
from jax import lax
from jax.experimental import pallas as pl
from jax.experimental.pallas import tpu as pltpu
from jax.sharding import PartitionSpec as P

TRAIN_STEP = 10
BETA_ONE = 0.9
BETA_TWO = 0.95
ADAM_EPS = 1e-8
NORM_EPS = 1e-6
LEARN_RATE = 0.003
STEP_SIZE = LEARN_RATE / (1.0 - BETA_ONE ** TRAIN_STEP)
VEL_GAIN = 1.0 / (1.0 - BETA_TWO ** TRAIN_STEP)
MESH = pl.DeviceIdType.MESH
NMAT = 4
F32 = jnp.float32
D = 1024
FF = 3072
HALF = 512
TILE = 256
HALF_SHAPE = ((64, 1024), (16, 1024), (8, 512))
CHUNK_ROWS = (128, 32, 8)
AXES = 3
RING = 4
BOTH = 2
NSET = 2


class Torus:
    def __init__(self):
        self.rep = lax.axis_index('rep')
        self.core = lax.axis_index('data')

    def stride(self, axis):
        return 1 + 3 * lax.rem(axis, 3) + 9 * lax.div(lax.rem(axis, 3), 2)

    def pos(self, axis):
        return lax.rem(lax.div(self.rep, self.stride(axis)), 4)

    def peer(self, axis, delta):
        stride = self.stride(axis)
        pos = lax.rem(lax.div(self.rep, stride), 4)
        return {'rep': self.rep + (lax.rem(pos + delta + 4, 4) - pos) * stride, 'data': self.core}


class Exchange:
    def __init__(self, tor, grads, slots, norm_buf, rs_send, rs_recv, ag_send, ag_recv, free_sem, slot_sem, nm_send, nm_recv):
        self.free_sem, self.slot_sem = free_sem, slot_sem
        self.tor, self.grads, self.slots = tor, grads, slots
        self.pos = [tor.pos(axis) for axis in range(AXES)]
        self.base = []
        for stream in range(AXES):
            base = stream * HALF
            for level in range(AXES):
                self.base.append(base)
                base = base + self.pos[(stream + level) % AXES] * CHUNK_ROWS[level]
        self.norm_buf = norm_buf
        self.rs_send, self.rs_recv, self.ag_send, self.ag_recv = rs_send, rs_recv, ag_send, ag_recv
        self.nm_send, self.nm_recv = nm_send, nm_recv

    def neighbour(self, stream, level, side):
        axis = (stream + level) % AXES
        pos = self.pos[axis]
        return {'rep': self.tor.rep + (lax.rem(pos + 1 + BOTH * side, RING) - pos) * RING ** axis, 'data': self.tor.core}

    def region(self, mat, stream, level, delta, half):
        rows = CHUNK_ROWS[level]
        row = self.base[stream * AXES + level] + lax.rem(self.pos[(stream + level) % AXES] + delta, RING) * rows
        if level < BOTH:
            row = pl.multiple_of(row + half * (rows // BOTH), rows // BOTH)
            return self.grads.at[mat, pl.ds(row, rows // BOTH), :]
        return self.grads.at[mat, pl.ds(pl.multiple_of(row, rows), rows), pl.ds(pl.multiple_of(half * HALF, HALF), HALF)]

    def rs_copy(self, mat, stream, level, msg, side):
        near = 1 + BOTH * side
        if isinstance(msg, int):
            delta, half = ((BOTH, side), (near, 1 - side), (near, side))[msg]
        else:
            delta, half = BOTH + msg * (near - BOTH), side + msg * (1 - BOTH * side)
        return pltpu.make_async_remote_copy(
            src_ref=self.region(mat, stream, level, delta, half),
            dst_ref=self.slots[level].at[lax.rem(mat, NSET), stream, msg, side],
            send_sem=self.rs_send.at[mat, level],
            recv_sem=self.rs_recv.at[mat, level, msg - msg // BOTH if isinstance(msg, int) else msg],
            device_id=self.neighbour(stream, level, side), device_id_type=MESH)

    def ag_copy(self, mat, stream, level, msg, side):
        if isinstance(msg, int):
            delta, half = ((0, side), (0, 1 - side), (RING - 1 - BOTH * side, side))[msg]
        else:
            delta, half = 0, side + msg * (1 - BOTH * side)
        ref = self.region(mat, stream, level, delta, half)
        return pltpu.make_async_remote_copy(
            src_ref=ref, dst_ref=ref,
            send_sem=self.ag_send.at[mat, level],
            recv_sem=self.ag_recv.at[mat, level, msg - msg // BOTH if isinstance(msg, int) else msg],
            device_id=self.neighbour(stream, level, side), device_id_type=MESH)

    def pairs(self, body, msgs=1):
        for stream in range(AXES):
            def one(idx, carry, stream=stream):
                body(stream, lax.rem(idx, BOTH), lax.div(idx, BOTH))
                return carry
            lax.fori_loop(0, BOTH * msgs, one, 0)

    def bulk(self, mat, level, late, gather):
        send, recv = (self.ag_send, self.ag_recv) if gather else (self.rs_send, self.rs_recv)
        count = AXES * BOTH * (AXES if late is None else 1 + late)
        rows = count * HALF_SHAPE[level][0] * HALF_SHAPE[level][1] // D
        ref = self.grads.at[mat, pl.ds(0, rows), :]
        copy = pltpu.make_async_remote_copy(src_ref=ref, dst_ref=ref, send_sem=send.at[mat, level], recv_sem=recv.at[mat, level, late or 0], device_id=self.neighbour(0, level, 0), device_id_type=MESH)
        if late is None:
            copy.wait_send()
        else:
            copy.wait_recv()

    def rs_first(self, mat, level):
        @pl.when(mat < NMAT - NSET)
        def _():
            pl.semaphore_wait(self.slot_sem.at[mat, level], AXES * BOTH)
        self.pairs(lambda stream, side, msg: self.rs_copy(mat, stream, level, msg, side).start(), BOTH)

    def rs_mid(self, mat, level):
        self.bulk(mat, level, 0, False)

        def body(stream, side, _):
            ref = self.region(mat, stream, level, 1 + BOTH * side, side)
            ref[...] = ref[...] + self.slots[level][lax.rem(mat, NSET), stream, 0, side]
            self.rs_copy(mat, stream, level, BOTH, side).start()
        self.pairs(body)

    def rs_last(self, mat, level):
        self.bulk(mat, level, 1, False)
        self.bulk(mat, level, None, False)

        def body(stream, half, _):
            ref = self.region(mat, stream, level, 0, half)
            held = self.slots[level]
            total = ref[...] + held[lax.rem(mat, NSET), stream, 2, half] + held[lax.rem(mat, NSET), stream, 1, 1 - half]
            if level == 2:
                total = total * (1.0 / 128.0)
                square = total * total
                self.norm_buf[4, 0] = self.norm_buf[4, 0] + sum(square[:, col * 128:(col + 1) * 128] for col in range(RING))
            ref[...] = total
        self.pairs(body)

        def tell(stream, side, _):
            peer = self.neighbour(stream, level, side)
            pl.semaphore_signal(self.free_sem.at[mat, level], inc=1, device_id=peer, device_id_type=MESH)

            @pl.when(mat >= NSET)
            def _():
                pl.semaphore_signal(self.slot_sem.at[mat - NSET, level], inc=1, device_id=peer, device_id_type=MESH)
        self.pairs(tell)

    def ag_first(self, mat, level):
        pl.semaphore_wait(self.free_sem.at[mat, level], AXES * BOTH)
        self.pairs(lambda stream, side, msg: self.ag_copy(mat, stream, level, msg, side).start(), BOTH)

    def ag_mid(self, mat, level):
        self.bulk(mat, level, 0, True)
        self.pairs(lambda stream, side, _: self.ag_copy(mat, stream, level, BOTH, side).start())

    def ag_last(self, mat, level):
        self.bulk(mat, level, 1, True)

    def step(self, mat, num):
        if num == 0:
            self.rs_first(mat, 0)
        elif num in (1, 3, 5):
            self.rs_mid(mat, num // 2)
        elif num in (2, 4):
            self.rs_last(mat, num // 2 - 1)
            self.rs_first(mat, num // 2)
        elif num == 6:
            self.rs_last(mat, 2)
            self.ag_first(mat, 2)
        elif num in (7, 9, 11):
            self.ag_mid(mat, 2 - (num - 7) // 2)
        elif num in (8, 10):
            level = 2 - (num - 8) // 2
            self.ag_last(mat, level)
            self.ag_first(mat, level - 1)
        else:
            self.ag_last(mat, 0)

    def norm_copy(self, stage, delta):
        tor = self.tor
        if stage < 3:
            mine, dev = tor.pos(stage), tor.peer(stage, delta)
        else:
            mine, dev = tor.core, {'data': 1 - tor.core}
        return pltpu.make_async_remote_copy(
            src_ref=self.norm_buf.at[4, stage], dst_ref=self.norm_buf.at[stage, mine],
            send_sem=self.nm_send.at[stage, delta], recv_sem=self.nm_recv.at[stage, delta],
            device_id=dev, device_id_type=MESH)

    def deltas(self, stage):
        return (1, 2, 3) if stage < AXES else (1,)

    def norm_start(self, stage):
        for delta in (self.deltas(stage)):
            self.norm_copy(stage, delta).start()
        mine = self.tor.pos(stage) if stage < 3 else self.tor.core
        self.norm_buf[stage, mine] = self.norm_buf[4, stage]

    def norm_finish(self, stage):
        for delta in (self.deltas(stage)):
            self.norm_copy(stage, delta).wait_recv()
        total = self.norm_buf[stage, 0] + self.norm_buf[stage, 1]
        if stage < 3:
            total = total + self.norm_buf[stage, 2] + self.norm_buf[stage, 3]
            self.norm_buf[4, stage + 1] = total
        else:
            self.norm_buf[4, 4] = total

    def drain(self):
        def one(mat, carry):
            for level in range(AXES):
                self.bulk(mat, level, None, True)
            return carry
        lax.fori_loop(0, NMAT, one, 0)
        for stage in range(4):
            for delta in (self.deltas(stage)):
                self.norm_copy(stage, delta).wait_send()

    def greet(self):
        tor = self.tor
        barrier = pltpu.get_barrier_semaphore()
        for axis in range(AXES):
            for delta in (1, 2, 3):
                pl.semaphore_signal(barrier, inc=1, device_id=tor.peer(axis, delta), device_id_type=MESH)
        pl.semaphore_signal(barrier, inc=1, device_id={'data': 1 - tor.core}, device_id_type=MESH)
        pl.semaphore_wait(barrier, 10)


SUB = 64
OCT = 8
LANE = 128
OWN = 1536
TILES = 6
HBM_ANY = pl.BlockSpec(memory_space=pl.ANY)
ROWS_ROWS = (((0,), (0,)), ((), ()))
COLS_COLS = (((1,), (1,)), ((), ()))
COMPUTE_SLOTS = 40
STEP_SLOTS = (
    (7, 11, 15, 17, 18, 22, 24, 25, 26, 31, 33, 46, 50),
    (17, 20, 24, 28, 40, 41, 43, 44, 45, 47, 50, 58, 64),
    (27, 31, 41, 42, 43, 44, 45, 46, 49, 55, 62, 72, 79),
    (39, 40, 41, 42, 43, 44, 45, 47, 60, 66, 76, 85, 92),
)
NORM_SLOTS = (45, 46, 47, 48, 50)
ADAM_RUNS = ((50, 48, 0),)
ADAM_READY = 42
LANES = 12
AHEAD = 8
PER_SLOT = 2
PIECES = 24
SLOTS = 98
GELU_A = 0.7978845608028654
GELU_B = 0.044715


def gelu_slope(hidden):
    square = hidden * hidden
    tanh = jnp.tanh(hidden * (GELU_A + GELU_A * GELU_B * square))
    return 0.5 * (1.0 + tanh) + (0.5 * hidden) * (1.0 - tanh * tanh) * (GELU_A + 3.0 * GELU_A * GELU_B * square)


N_ACTS = 11
N_STATE = 3


def take(refs, count, start=0):
    return refs[start:start + count]


def backward_kernel(*refs):
    x_in, dy_in, w_two, w_three, w_four, h_one, a_one, y_one, h_two, a_two, clip_ref = take(refs, N_ACTS)
    masters, moms, vels = (take(refs, NMAT, N_ACTS + which * NMAT) for which in range(N_STATE))
    outs = refs[N_ACTS + N_STATE * NMAT:]
    new_w, new_masters, new_moms, new_vels = (take(outs, NMAT, which * NMAT) for which in range(NMAT))
    norm_ref, x_peer, a_one_peer, a_two_peer = take(outs, NMAT, NMAT * NMAT)
    (grads, slot_big, slot_mid, slot_low, norm_buf, scale_ref, dh_own, dh_peer, dy_pair, y_pair, a_tile, w_tile, h_tile,
     rs_send, rs_recv, ag_send, ag_recv, free_sem, slot_sem, nm_send, nm_recv,
     a_tile_sem, w_tile_sem, h_tile_sem, load_sem, dyx_sem, yx_sem, xx_sem, a_one_sem, a_two_sem, dh_sem, dyp_sem,
     in_sem, out_sem, w_send, w_recv) = outs[NMAT * NMAT + NMAT:]
    tor = Torus()
    ex = Exchange(tor, grads, (slot_big, slot_mid, slot_low), norm_buf, rs_send, rs_recv, ag_send, ag_recv, free_sem, slot_sem, nm_send, nm_recv)
    core = tor.core
    other = 1 - core
    mate = {'data': other}

    def send(src, dst, sem):
        return pltpu.make_async_remote_copy(src_ref=src, dst_ref=dst, send_sem=sem.at[0], recv_sem=sem.at[1], device_id=mate, device_id_type=MESH)

    def columns(start, size):
        return pl.ds(pl.multiple_of(start, size), size)

    def piece_rows(index, base=0):
        return pl.ds(pl.multiple_of(base + index * SUB, SUB), SUB)

    dy_swap = send(dy_in, dy_pair.at[pl.ds(D, D), :], dyx_sem)
    y_swap = send(y_one.at[:, columns(other * HALF, HALF)], y_pair.at[pl.ds(D, D), :], yx_sem)
    x_swap = send(x_in.at[:, columns(other * HALF, HALF)], x_peer, xx_sem)

    def a_swap(layer, tile):
        src, dst, sem = ((a_one, a_one_peer, a_one_sem), (a_two, a_two_peer, a_two_sem))[layer]
        return send(src.at[:, columns(other * OWN + tile * TILE, TILE)], dst.at[:, columns(tile * TILE, TILE)], sem.at[tile])

    def dh_swap(layer, tile):
        return send(dh_own.at[:, columns(tile * HALF, HALF)], dh_peer.at[:, columns(tile * HALF, HALF)], dh_sem.at[layer, tile])

    def dyp_swap(tile):
        return send(dy_pair.at[pl.ds(0, D), columns(tile * TILE, TILE)], dy_pair.at[pl.ds(D, D), columns(tile * TILE, TILE)], dyp_sem.at[tile])

    def a_load(layer, tile, part):
        slot = lax.rem(tile, BOTH)
        if part == 0:
            src = (a_one, a_two)[layer].at[:, columns(core * OWN + tile * TILE, TILE)]
        else:
            src = (a_one_peer, a_two_peer)[layer].at[:, columns(tile * TILE, TILE)]
        return pltpu.make_async_copy(src, a_tile.at[slot, pl.ds(part * D, D), :], a_tile_sem.at[slot, part])

    def w_load(layer, tile):
        slot = lax.rem(tile, BOTH)
        src = (w_two, w_four)[layer].at[pl.ds(pl.multiple_of(tile * HALF, HALF), HALF), :]
        return [pltpu.make_async_copy(src.at[pl.ds(part * TILE, TILE), :], w_tile.at[slot, :, pl.ds(part * D, D)], w_tile_sem.at[slot, part]) for part in range(2)]

    def w_three_load(tile):
        slot = lax.rem(tile, BOTH)
        return [pltpu.make_async_copy(w_three.at[pl.ds(pl.multiple_of(tile * TILE, TILE), TILE), :], w_tile.at[slot], w_tile_sem.at[slot, 0])]

    def h_load(layer, tile):
        slot = lax.rem(tile, BOTH)
        return pltpu.make_async_copy((h_one, h_two)[layer].at[:, columns(tile * HALF, HALF)], h_tile.at[slot], h_tile_sem.at[slot])

    def start_all(copies):
        for copy in copies:
            copy.start()

    def wait_all(copies):
        for copy in copies:
            copy.wait()

    dy_load = pltpu.make_async_copy(dy_in, dy_pair.at[pl.ds(0, D), :], load_sem.at[0])
    y_load = pltpu.make_async_copy(y_one.at[:, columns(core * HALF, HALF)], y_pair.at[pl.ds(0, D), :], load_sem.at[1])
    x_load = pltpu.make_async_copy(x_in.at[:, columns(core * HALF, HALF)], y_pair.at[pl.ds(0, D), :], load_sem.at[2])
    x_peer_load = pltpu.make_async_copy(x_peer, y_pair.at[pl.ds(D, D), :], load_sem.at[3])

    dy_load.start()
    start_all(w_load(1, 0))
    h_load(1, 0).start()
    a_load(1, 0, 0).start()
    y_load.start()
    ex.greet()
    dy_swap.start()
    for layer in (1, 0):
        def swap_one(tile, carry, layer=layer):
            a_swap(layer, tile).start()
            return carry
        lax.fori_loop(0, TILES, swap_one, 0)
        if layer == 1:
            y_swap.start()
    x_swap.start()
    norm_buf[4, 0] = jnp.zeros((OCT, LANE), F32)
    dy_load.wait()

    def dh_slot(layer, tile):
        slot = lax.rem(tile, BOTH)

        @pl.when(tile < TILES - 1)
        def _():
            start_all(w_load(layer, tile + 1))
            h_load(layer, tile + 1).start()

        if layer == 1:
            @pl.when(tile == TILES - 1)
            def _():
                start_all(w_three_load(0))
        wait_all(w_load(layer, tile))
        h_load(layer, tile).wait()
        def part_body(part, carry):
            rows = pl.ds(pl.multiple_of(part * HALF, HALF), HALF)
            for half in range(2):
                acc = lax.dot_general(dy_pair[rows, :], w_tile[slot, :, half * D:(half + 1) * D], COLS_COLS, preferred_element_type=F32)
                slope = gelu_slope(h_tile[slot, rows, half * TILE:(half + 1) * TILE].astype(F32))
                dh_own[rows, columns(tile * HALF + half * TILE, TILE)] = (slope * acc.astype(jnp.bfloat16).astype(F32)).astype(jnp.bfloat16)
            return carry
        lax.fori_loop(0, BOTH, part_body, 0)
        dh_swap(layer, tile).start()

    def row_slot(layer, tile):
        slot = lax.rem(tile, BOTH)

        @pl.when(tile == 0)
        def _():
            if layer == 1:
                dy_swap.wait()
                y_swap.wait_send()
            else:
                for part in range(4):
                    dyp_swap(part).wait()
            a_swap(layer, tile).wait()
            a_load(layer, tile, 1).start()

        @pl.when(tile < TILES - 1)
        def _():
            a_load(layer, tile + 1, 0).start()
            a_swap(layer, tile + 1).wait()
            a_load(layer, tile + 1, 1).start()
        a_load(layer, tile, 0).wait()
        a_load(layer, tile, 1).wait()
        grads[1 + 2 * layer, pl.ds(pl.multiple_of(tile * TILE, TILE), TILE), :] = lax.dot_general(a_tile[slot], dy_pair[...], ROWS_ROWS, preferred_element_type=F32)

    def column_slot(layer, tile):
        @pl.when(tile == 0)
        def _():
            if layer == 1:
                y_load.wait()
                y_swap.wait_recv()
            else:
                x_load.wait()
                x_peer_load.wait()
        dh_swap(layer, tile).wait()
        cols = columns(tile * HALF, HALF)

        def part_body(part, carry):
            mine = columns(part * TILE, TILE)
            total = lax.dot_general(y_pair[0:D, mine], dh_own[:, cols], ROWS_ROWS, preferred_element_type=F32)
            total = total + lax.dot_general(y_pair[D:BOTH * D, mine], dh_peer[:, cols], ROWS_ROWS, preferred_element_type=F32)
            rows = pl.ds(pl.multiple_of(lax.div(tile, 2) * HALF + part * TILE, TILE), TILE)
            grads[2 * layer, rows, columns(lax.rem(tile, BOTH) * HALF, HALF)] = total
            return carry
        lax.fori_loop(0, BOTH, part_body, 0)

    def dy_slot(tile):
        slot = lax.rem(tile, BOTH)

        @pl.when(tile < 3)
        def _():
            start_all(w_three_load(tile + 1))

        @pl.when(tile == 3)
        def _():
            start_all(w_load(0, 0))
            h_load(0, 0).start()
            a_load(0, 0, 0).start()
            x_load.start()
            x_swap.wait()
            x_peer_load.start()
        wait_all(w_three_load(tile))
        acc = lax.dot_general(dh_own[...], w_tile[slot], COLS_COLS, preferred_element_type=F32)
        dy_pair[0:D, columns(tile * TILE, TILE)] = acc.astype(jnp.bfloat16)
        dyp_swap(tile).start()

    def lane_tile(item, which):
        lane = lax.rem(item, LANES)
        return slot_big.at[lax.div(lane, 6), lax.rem(lax.div(lane, 2), 3), which, lax.rem(lane, 2)]

    def w_stage(item):
        return dh_own.at[piece_rows(lax.rem(item, LANES)), 0:D]

    def state_view(ref, mat, piece):
        if mat in (1, 3):
            return ref.at[piece_rows(piece), :]
        return ref.at[piece_rows(lax.rem(piece, OCT)), columns(lax.div(piece, OCT) * D, D)]

    def w_view(mat, piece):
        ref = new_w[mat]
        if mat in (1, 3):
            return ref.at[piece_rows(piece, core * OWN), :]
        return ref.at[piece_rows(lax.rem(piece, OCT), core * HALF), columns(lax.div(piece, OCT) * D, D)]

    def state_load(item, which, mat, piece):
        return pltpu.make_async_copy(state_view((moms, vels, masters)[which][mat], mat, piece), lane_tile(item, which), in_sem.at[lax.rem(item, LANES), which])

    def state_store(item, which, mat, piece):
        return pltpu.make_async_copy(lane_tile(item, which), state_view((new_moms, new_vels, new_masters)[which][mat], mat, piece), out_sem.at[lax.rem(item, LANES), which])

    def w_store(item, mat, piece):
        return pltpu.make_async_copy(w_stage(item), w_view(mat, piece), out_sem.at[lax.rem(item, LANES), N_STATE])

    def w_swap(item, mat, piece):
        return pltpu.make_async_remote_copy(src_ref=w_stage(item), dst_ref=w_view(mat, piece), send_sem=w_send.at[lax.rem(item, LANES)], recv_sem=w_recv.at[item], device_id=mate, device_id_type=MESH)

    def piece_of(item):
        idx = lax.rem(item, PIECES)
        early = idx < 12
        rest = idx - 12
        stream = jnp.where(early, lax.div(lax.rem(idx, 6), BOTH), lax.div(rest, RING))
        odd = lax.rem(idx, BOTH)
        far = lax.div(lax.rem(rest + 12, RING), BOTH)
        delta = jnp.where(idx < 6, 0, jnp.where(early, 3 - BOTH * odd, jnp.where(far == 1, BOTH, 3 - BOTH * odd)))
        half = jnp.where(early, odd, jnp.where(far == 1, odd, 1 - odd))
        pos = jnp.where(stream == 0, ex.pos[0], jnp.where(stream == 1, ex.pos[1], ex.pos[2]))
        return stream * OCT + lax.rem(pos + delta, RING) * BOTH + half

    def for_mat(item, body):
        place = lax.div(item, PIECES)
        piece = piece_of(item)
        for which in range(NMAT):
            @pl.when(place == which)
            def _(which=which):
                body(NMAT - 1 - which, piece)

    def adam_fetch(item):
        def body(mat, piece):
            for which in range(N_STATE):
                state_load(item, which, mat, piece).start()
        for_mat(item, body)

    def adam_flush(item):
        for which in range(N_STATE):
            state_store(item, which, 1, 0).wait()
        w_store(item, 1, 0).wait()
        w_swap(item, 1, 0).wait_send()

    def adam_item(item):
        @pl.when(item >= LANES - AHEAD)
        def _():
            adam_flush(item - (LANES - AHEAD))

        @pl.when(item < NMAT * PIECES - AHEAD)
        def _():
            adam_fetch(item + AHEAD)
        for which in range(N_STATE):
            state_load(item, which, 1, 0).wait()
        mom, vel, master = (lane_tile(item, which) for which in range(N_STATE))
        mat, piece = NMAT - 1 - lax.div(item, PIECES), piece_of(item)
        scaled = scale_ref[0:1, 0:1] * grads[mat, piece_rows(piece), :]
        mom_new = BETA_ONE * mom[...] + (1.0 - BETA_ONE) * scaled
        vel_new = BETA_TWO * vel[...] + (1.0 - BETA_TWO) * jnp.square(scaled)
        master_new = master[...] - STEP_SIZE * mom_new / (jnp.sqrt(vel_new * VEL_GAIN) + ADAM_EPS)
        mom[...] = mom_new
        vel[...] = vel_new
        master[...] = master_new
        w_stage(item)[...] = master_new.astype(jnp.bfloat16)

        def body(mat, piece):
            for which in range(N_STATE):
                state_store(item, which, mat, piece).start()
            w_store(item, mat, piece).start()
            w_swap(item, mat, piece).start()
        for_mat(item, body)

    def set_scale():
        total = jnp.sum(jnp.sum(norm_buf[NMAT, NMAT], axis=0, keepdims=True), axis=1, keepdims=True)
        norm = jnp.sqrt(total)
        norm_ref[...] = jnp.broadcast_to(norm, norm_ref.shape)
        scale_ref[...] = jnp.broadcast_to(jnp.minimum(1.0, clip_ref[...] / (norm + NORM_EPS)), scale_ref.shape)

    def during(first, last, now, body):
        @pl.when((now >= first) & (now < last))
        def _():
            body()

    def compute(now):
        during(0, 2, now, lambda: dh_slot(1, now))
        during(2, 8, now, lambda: row_slot(1, now - 2))
        during(8, 12, now, lambda: dh_slot(1, now - 6))
        during(12, 18, now, lambda: column_slot(1, now - 12))
        during(18, 22, now, lambda: dy_slot(now - 18))
        during(22, 28, now, lambda: row_slot(0, now - 22))
        during(28, 34, now, lambda: dh_slot(0, now - 28))
        during(34, 40, now, lambda: column_slot(0, now - 34))

    def late(now):
        for stage in range(NMAT + 1):
            @pl.when(now == NORM_SLOTS[stage])
            def _(stage=stage):
                if stage > 0:
                    ex.norm_finish(stage - 1)
                if stage < NMAT:
                    ex.norm_start(stage)
                else:
                    set_scale()

        @pl.when(now == ADAM_READY)
        def _():
            for item in range(AHEAD):
                adam_fetch(item)

        first = 0
        active = 0
        for start, length, chunk in ADAM_RUNS:
            inside = (now >= start) & (now < start + length)
            first = jnp.where(inside, (now - start + chunk) * PER_SLOT, first)
            active = jnp.where(inside, 1, active)

        @pl.when(active == 1)
        def _():
            def adam_body(idx, carry):
                adam_item(first + idx)
                return carry
            lax.fori_loop(0, PER_SLOT, adam_body, 0)

    def slot_body(now, carry):
        @pl.when(now < COMPUTE_SLOTS)
        def _():
            compute(now)

        nums = []
        for which in range(NMAT):
            num = -1
            for order, at in enumerate(STEP_SLOTS[which]):
                num = jnp.where(now == at, order, num)
            nums.append(num)

        def place_body(place, c2):
            num = nums[0]
            for which in range(1, NMAT):
                num = jnp.where(place == which, nums[which], num)
            mat = NMAT - 1 - place

            @pl.when(num >= 0)
            def _():
                for want in range(13):
                    @pl.when(num == want)
                    def _(want=want):
                        ex.step(mat, want)
            return c2
        most = jnp.maximum(jnp.maximum(nums[0], nums[1]), jnp.maximum(nums[2], nums[3]))

        @pl.when(most >= 0)
        def _():
            lax.fori_loop(0, NMAT, place_body, 0)

        @pl.when(now >= COMPUTE_SLOTS)
        def _():
            late(now)
        return carry

    lax.fori_loop(0, SLOTS, slot_body, 0)
    for item in range(NMAT * PIECES - (LANES - AHEAD), NMAT * PIECES):
        adam_flush(item)

    def w_wait(item, carry):
        w_swap(item, 1, 0).wait_recv()
        return carry
    lax.fori_loop(0, NMAT * PIECES, w_wait, 0)
    ex.drain()


def backward(acts, clip_norm, masters, moms, vels):
    bf16 = jnp.bfloat16
    sds = jax.ShapeDtypeStruct
    dma = pltpu.SemaphoreType.DMA
    whole = [sds((D, FF), bf16), sds((FF, D), bf16)]
    rows = [sds((HALF, FF), F32), sds((OWN, D), F32)]
    in_vmem = pl.BlockSpec(memory_space=pltpu.VMEM)
    outs = pl.pallas_call(
        backward_kernel,
        out_shape=whole * 2 + rows * 6 + [sds((OCT, LANE), F32), sds((D, HALF), bf16), sds((D, OWN), bf16), sds((D, OWN), bf16)],
        in_specs=[HBM_ANY] * (N_ACTS - 1) + [in_vmem] + [HBM_ANY] * (N_STATE * NMAT),
        out_specs=[HBM_ANY] * (NMAT * NMAT) + [in_vmem] + [HBM_ANY] * N_STATE,
        scratch_shapes=[
            pltpu.VMEM((NMAT, OWN, D), F32),
            pltpu.VMEM((NSET, AXES, AXES, BOTH) + HALF_SHAPE[0], F32),
            pltpu.VMEM((NSET, AXES, AXES, BOTH) + HALF_SHAPE[1], F32),
            pltpu.VMEM((NSET, AXES, AXES, BOTH) + HALF_SHAPE[2], F32),
            pltpu.VMEM((NMAT + 1, NMAT + 1, OCT, LANE), F32),
            pltpu.VMEM((OCT, LANE), F32),
            pltpu.VMEM((D, FF), bf16),
            pltpu.VMEM((D, FF), bf16),
            pltpu.VMEM((BOTH * D, D), bf16),
            pltpu.VMEM((BOTH * D, HALF), bf16),
            pltpu.VMEM((2, BOTH * D, TILE), bf16),
            pltpu.VMEM((2, TILE, FF), bf16),
            pltpu.VMEM((2, D, HALF), bf16),
            dma((NMAT, AXES)),
            dma((NMAT, AXES, BOTH)),
            dma((NMAT, AXES)),
            dma((NMAT, AXES, BOTH)),
            pltpu.SemaphoreType.REGULAR((NMAT, AXES)),
            pltpu.SemaphoreType.REGULAR((NMAT, AXES)),
            dma((4, 4)),
            dma((4, 4)),
            dma((2, 2)),
            dma((2, 3)),
            dma((BOTH,)),
            dma((4,)),
            dma((BOTH,)),
            dma((BOTH,)),
            dma((BOTH,)),
            dma((TILES, BOTH)),
            dma((TILES, BOTH)),
            dma((2, 6, 2)),
            dma((4, 2)),
            dma((LANES, 3)),
            dma((LANES, 4)),
            dma((LANES,)),
            dma((NMAT * PIECES,)),
        ],
        compiler_params=pltpu.CompilerParams(collective_id=0, has_side_effects=True, vmem_limit_bytes=67043328),
        name='backward_exchange',
    )(*acts, clip_norm.reshape(1, 1), *masters, *moms, *vels)
    return outs[:NMAT * NMAT], outs[NMAT * NMAT]


def gelu_fn(values):
    return jax.nn.gelu(values, approximate=True)


def forward(act_in, w_one, w_two, w_three):
    bf16 = jnp.bfloat16
    h_one = jnp.dot(act_in, w_one, preferred_element_type=F32).astype(bf16)
    a_one = gelu_fn(h_one.astype(F32)).astype(bf16)
    y_one = jnp.dot(a_one, w_two, preferred_element_type=F32).astype(bf16)
    h_two = jnp.dot(y_one, w_three, preferred_element_type=F32).astype(bf16)
    a_two = gelu_fn(h_two.astype(F32)).astype(bf16)
    return h_one, a_one, y_one, h_two, a_two


def solution(mesh):
    row_spec = P(('rep', 'data'), None)
    shard_spec = P('data', None)
    full_spec = P()

    def per_device(act_in, grad_out, w_one, w_two, w_three, w_four, master_one, master_two, master_three, master_four, mom_one, mom_two, mom_three, mom_four, vel_one, vel_two, vel_three, vel_four, clip_norm):
        h_one, a_one, y_one, h_two, a_two = forward(act_in, w_one, w_two, w_three)
        acts = (act_in, grad_out, w_two, w_three, w_four, h_one, a_one, y_one, h_two, a_two)
        new_state, norm_block = backward(acts, clip_norm, (master_one, master_two, master_three, master_four), (mom_one, mom_two, mom_three, mom_four), (vel_one, vel_two, vel_three, vel_four))
        return tuple(new_state) + (norm_block[0, 0],)

    in_specs = (row_spec, row_spec, full_spec, full_spec, full_spec, full_spec) + (shard_spec,) * 12 + (full_spec,)
    out_specs = (full_spec,) * 4 + (shard_spec,) * 12 + (full_spec,)
    return jax.shard_map(per_device, mesh=mesh, in_specs=in_specs, out_specs=out_specs, check_vma=False)
```

time: 638 us -> 338 us (0.53); the launches traced: 629 us -> 338 us
  waiting for transfers between devices: 295 us -> 0 us
  Pallas kernels: 0 us -> 232 us
  matrix products: 119 us -> 31.7 us
  other arithmetic: 80.1 us -> 0.01 us
  local copies, waits for them, and re-layouts: 110 us -> 73 us
  between operations: 19.5 us -> 1.45 us
    psum x1 -> x0, waiting for transfers between devices: 260 us -> none  [per_device(): reduced[mat_idx] = lax.psum(row_part, 'rep') / dev_count]
    pallas_call x0 -> x1, Pallas kernels: none -> 232 us  [backward(): pl.pallas_call(backward_kernel, out_shape=whole * 2 + rows * 6 + [sds((OC...]
    dot_general x9 -> x3, matrix products: 119 us -> 31.7 us  [the longest x1 13.1 us: forward(): h_one = jnp.dot(act_in, w_one, preferred_element_type=F32).astype(bf16)]
    convert_element_type x4 -> x0, other arithmetic: 70.8 us -> none  [per_device(): upd_set[0].astype(jnp.bfloat16)]
    unnamed x40 -> x74, local copies, waits for them, and re-layouts: 110 us -> 71.8 us
    reduce_scatter x4 -> x0, waiting for transfers between devices: 34.8 us -> none  [per_device(): lax.psum_scatter(local_list[mat_idx], 'data', scatter_dimension=0, tiled=...]
    reduce_sum x2 -> x0, other arithmetic: 9.31 us -> none  [per_device(): jnp.sum(jnp.square(reduced[mat_idx]))]
  transfers between devices with their start and end apart: 9 -> 0, of which waited for: 3 -> 0; matrix products, arithmetic and copies ran while one was open for 33% -> 0% of each run, Pallas kernels for 0% -> 0%
where the time goes in v1:
time: 338 us
  Pallas kernels  232 us (69%)
  local copies, waits for them, and re-layouts  73 us (22%)
  matrix products  31.7 us (9%)
    pallas_call x1, Pallas kernels, backward(): pl.pallas_call(backward_kernel, out_shape=whole * 2 + rows * 6 + [sds((OC...  232 us
    unnamed x74, local copies, waits for them, and re-layouts  71.8 us
    dot_general x1, matrix products, forward(): h_one = jnp.dot(act_in, w_one, preferred_element_type=F32).astype(bf16)  13.1 us
    dot_general x1, matrix products, forward(): h_two = jnp.dot(y_one, w_three, preferred_element_type=F32).astype(bf16)  11.7 us
    dot_general x1, matrix products, forward(): y_one = jnp.dot(a_one, w_two, preferred_element_type=F32).astype(bf16)  6.87 us

profile of v1, /device:TPU:1, one launch (start us, length us, event | category | flops | bytes accessed | tf_op | source)
XLA Modules:
  0.0 337.9 jit_solution(1228178852089408308)
XLA Ops:
  1.3 0.0 copy-start
  1.3 13.1 %fusion.5 = (bf16[1024,3072]{1,0:T(8,128)(2,1)S(1)}, bf16[1024,3072]{1,0:T(8,128)(2,1)}) fusion(bf16[1024,1024]{1,0:T(8,128)(2,1)} %refs_0_.1, bf16[1024,3072]{1,0:T(8,128)(2,1)} %param.21), kind=kOutput, calls=%fused_computation.13 | convolution fusion | flops 6477053952 | bytes 20971520 | tf_op jit(solution)/shard_map/dot_general | solution.py:709
  14.4 0.0 copy-done
  14.4 6.9 %fusion.13.refs_7_ = bf16[1024,1024]{1,0:T(8,128)(2,1)S(1)} fusion(bf16[1024,3072]{1,0:T(8,128)(2,1)S(1)} %get-tuple-element.51.refs_6_, bf16[3072,1024]{1,0:T(8,128)(2,1)S(1)} %copy-done), kind=kOutput, calls=%fused_computation.23 | convolution fusion | flops 6442450944 | bytes 14680064 | tf_op jit(solution)/shard_map/dot_general | solution.py:711
  21.3 0.0 copy-done.2
  21.3 0.0 copy-done.1
  21.3 0.0 copy-start.4
  21.3 11.7 %fusion.11 = (bf16[1024,3072]{1,0:T(8,128)(2,1)}, bf16[1024,3072]{1,0:T(8,128)(2,1)}) fusion(bf16[1024,1024]{1,0:T(8,128)(2,1)S(1)} %fusion.13.refs_7_, bf16[1024,3072]{1,0:T(8,128)(2,1)S(1)} %copy-done.1), kind=kOutput, calls=%fused_computation.19 | convolution fusion | flops 6477053952 | bytes 20971520 | tf_op jit(solution)/shard_map/dot_general | solution.py:712
  33.0 0.0 copy-done.4
  33.0 231.8 %backward_exchange.1 = (bf16[1024,3072]{1,0:T(8,128)(2,1)}, bf16[3072,1024]{1,0:T(8,128)(2,1)}, bf16[1024,3072]{1,0:T(8,128)(2,1)}, bf16[3072,1024]{1,0:T(8,128)...) custom-call(bf16[1024,1024]{1,0:T(8,128)(2,1)} %refs_0_.1, ...), custom_call_target="tpu_custom_call" | custom-call | tf_op jit(solution)/shard_map/backward_exchange/pallas_call | solution.py:654
  264.8 1.2 slice.3
  266.0 6.6 %copy.53 = bf16[1024,3072]{1,0:T(8,128)(2,1)} copy(bf16[1024,3072]{1,0:T(8,128)(2,1)} %get-tuple-element.72) | data formatting | bytes 12582912
  272.6 0.0 copy-done.3
  272.7 3.2 copy.54
  275.8 0.0 slice-done.22
  275.9 1.3 slice-done.23
  277.2 2.7 copy.55
  279.9 6.5 %copy.56 = bf16[3072,1024]{1,0:T(8,128)(2,1)} copy(bf16[3072,1024]{1,0:T(8,128)(2,1)} %get-tuple-element.75) | data formatting | bytes 12582912
  286.3 6.4 %copy.57 = f32[512,3072]{1,0:T(8,128)} copy(f32[512,3072]{1,0:T(8,128)} %get-tuple-element.76) | data formatting | bytes 12582912
  292.7 0.0 slice-done.20
  292.7 0.0 slice-done.21
  292.7 0.0 slice-start.14
  292.8 3.2 copy.58
  296.0 0.0 slice-done.18
  296.0 0.0 slice-done.19
  296.0 0.0 slice-start.15
  296.0 3.2 copy.59
  299.2 0.0 slice-done.16
  299.2 2.4 slice-done.17
  301.6 3.2 copy.60
  304.8 0.0 slice-done.14
  304.8 0.0 slice-start.11
  304.8 3.2 copy.61
  308.0 0.0 slice-done.12
  308.0 2.3 slice-done.13
  310.3 3.2 copy.62
  313.5 0.0 slice-done.11
  313.5 0.0 slice-start.7
  313.5 3.2 copy.63
  316.7 2.3 slice-done.9
  319.1 3.2 copy.64
  322.3 0.0 slice-start.3
  322.3 3.2 copy.65
  325.5 2.3 slice-done.5
  327.8 3.2 copy.66
  331.0 3.1 copy.67
  334.1 1.1 slice-done.1
  335.2 2.7 copy.68
  (43 shorter events, 0.1 us)
Async XLA Ops:
  1.3 13.1 %copy-start = (bf16[3072,1024]{1,0:T(8,128)(2,1)S(1)}, bf16[3072,1024]{1,0:T(8,128)(2,1)}, u32[]{:S(2)}) copy-start(bf16[3072,1024]{1,0:T(8,128)(2,1)} %refs_2_.1) | copy-start | bytes 18874372
  14.4 6.9 %copy-start.2 = (bf16[1024,3072]{1,0:T(8,128)(2,1)}, bf16[1024,3072]{1,0:T(8,128)(2,1)S(1)}, u32[]{:S(2)}) copy-start(bf16[1024,3072]{1,0:T(8,128)(2,1)S(1)} %get-tuple-element.51.refs_6_) | copy-start | bytes 18874372
  14.4 6.9 %copy-start.1 = (bf16[1024,3072]{1,0:T(8,128)(2,1)S(1)}, bf16[1024,3072]{1,0:T(8,128)(2,1)}, u32[]{:S(2)}) copy-start(bf16[1024,3072]{1,0:T(8,128)(2,1)} %refs_3_.1) | copy-start | bytes 18874372
  21.3 11.7 %copy-start.4 = (bf16[1024,1024]{1,0:T(8,128)(2,1)}, bf16[1024,1024]{1,0:T(8,128)(2,1)S(1)}, u32[]{:S(2)}) copy-start(bf16[1024,1024]{1,0:T(8,128)(2,1)S(1)} %fusion.13.refs_7_) | copy-start | bytes 6291460
  266.0 6.6 %copy-start.3 = (bf16[3072,1024]{1,0:T(8,128)(2,1)S(1)}, bf16[3072,1024]{1,0:T(8,128)(2,1)}, u32[]{:S(2)}) copy-start(bf16[3072,1024]{1,0:T(8,128)(2,1)} %get-tuple-element.73) | copy-start | bytes 18874372
  266.0 9.8 %slice-start.22 = ((s8[6291456]{0:T(1024)(128)(4,1)}), s8[4194304]{0:T(1024)(128)(4,1)S(1)}, s32[]{:S(2)}) async-start(s8[6291456]{0:T(1024)(128)(4,1)} %bitcast.31), calls=%async_computation.22 | async-start | bytes 8388608
  272.7 4.5 %slice-start.23 = ((s8[6291456]{0:T(1024)(128)(4,1)}), s8[2097152]{0:T(1024)(128)(4,1)S(1)}, s32[]{:S(2)}) async-start(s8[6291456]{0:T(1024)(128)(4,1)} %bitcast.31), calls=%async_computation.23 | async-start | bytes 4194304
  279.9 12.9 %slice-start.20 = ((s8[6291456]{0:T(1024)(128)(4,1)}), s8[4194304]{0:T(1024)(128)(4,1)S(1)}, s32[]{:S(2)}) async-start(s8[6291456]{0:T(1024)(128)(4,1)} %bitcast.29), calls=%async_computation.20 | async-start | bytes 8388608
  279.9 16.1 %slice-start.18 = ((s8[6291456]{0:T(1024)(128)(4,1)}), s8[4194304]{0:T(1024)(128)(4,1)S(1)}, s32[]{:S(2)}) async-start(s8[6291456]{0:T(1024)(128)(4,1)} %bitcast.27), calls=%async_computation.18 | async-start | bytes 8388608
  286.3 6.4 %slice-start.21 = ((s8[6291456]{0:T(1024)(128)(4,1)}), s8[2097152]{0:T(1024)(128)(4,1)S(1)}, s32[]{:S(2)}) async-start(s8[6291456]{0:T(1024)(128)(4,1)} %bitcast.29), calls=%async_computation.21 | async-start | bytes 4194304
  286.3 9.6 %slice-start.19 = ((s8[6291456]{0:T(1024)(128)(4,1)}), s8[2097152]{0:T(1024)(128)(4,1)S(1)}, s32[]{:S(2)}) async-start(s8[6291456]{0:T(1024)(128)(4,1)} %bitcast.27), calls=%async_computation.19 | async-start | bytes 4194304
  292.7 6.4 %slice-start.16 = ((s8[6291456]{0:T(1024)(128)(4,1)}), s8[4194304]{0:T(1024)(128)(4,1)S(1)}, s32[]{:S(2)}) async-start(s8[6291456]{0:T(1024)(128)(4,1)} %bitcast.25), calls=%async_computation.16 | async-start | bytes 8388608
  292.7 12.0 %slice-start.14 = ((s8[6291456]{0:T(1024)(128)(4,1)}), s8[4194304]{0:T(1024)(128)(4,1)S(1)}, s32[]{:S(2)}) async-start(s8[6291456]{0:T(1024)(128)(4,1)} %bitcast.23), calls=%async_computation.14 | async-start | bytes 8388608
  296.0 5.6 %slice-start.17 = ((s8[6291456]{0:T(1024)(128)(4,1)}), s8[2097152]{0:T(1024)(128)(4,1)S(1)}, s32[]{:S(2)}) async-start(s8[6291456]{0:T(1024)(128)(4,1)} %bitcast.25), calls=%async_computation.17 | async-start | bytes 4194304
  296.0 8.8 %slice-start.15 = ((s8[6291456]{0:T(1024)(128)(4,1)}), s8[2097152]{0:T(1024)(128)(4,1)S(1)}, s32[]{:S(2)}) async-start(s8[6291456]{0:T(1024)(128)(4,1)} %bitcast.23), calls=%async_computation.15 | async-start | bytes 4194304
  301.6 6.4 %slice-start.12 = ((s8[6291456]{0:T(1024)(128)(4,1)}), s8[4194304]{0:T(1024)(128)(4,1)S(1)}, s32[]{:S(2)}) async-start(s8[6291456]{0:T(1024)(128)(4,1)} %bitcast.21), calls=%async_computation.12 | async-start | bytes 8388608
  301.6 11.9 %slice-start.10 = ((s8[6291456]{0:T(1024)(128)(4,1)}), s8[4194304]{0:T(1024)(128)(4,1)S(1)}, s32[]{:S(2)}) async-start(s8[6291456]{0:T(1024)(128)(4,1)} %bitcast.19), calls=%async_computation.10 | async-start | bytes 8388608
  304.8 5.5 %slice-start.13 = ((s8[6291456]{0:T(1024)(128)(4,1)}), s8[2097152]{0:T(1024)(128)(4,1)S(1)}, s32[]{:S(2)}) async-start(s8[6291456]{0:T(1024)(128)(4,1)} %bitcast.21), calls=%async_computation.13 | async-start | bytes 4194304
  304.8 8.7 %slice-start.11 = ((s8[6291456]{0:T(1024)(128)(4,1)}), s8[2097152]{0:T(1024)(128)(4,1)S(1)}, s32[]{:S(2)}) async-start(s8[6291456]{0:T(1024)(128)(4,1)} %bitcast.19), calls=%async_computation.11 | async-start | bytes 4194304
  310.3 6.4 %slice-start.8 = ((s8[6291456]{0:T(1024)(128)(4,1)}), s8[4194304]{0:T(1024)(128)(4,1)S(1)}, s32[]{:S(2)}) async-start(s8[6291456]{0:T(1024)(128)(4,1)} %bitcast.17), calls=%async_computation.8 | async-start | bytes 8388608
  310.3 11.9 %slice-start.6 = ((s8[6291456]{0:T(1024)(128)(4,1)}), s8[4194304]{0:T(1024)(128)(4,1)S(1)}, s32[]{:S(2)}) async-start(s8[6291456]{0:T(1024)(128)(4,1)} %bitcast.15), calls=%async_computation.6 | async-start | bytes 8388608
  313.5 5.5 %slice-start.9 = ((s8[6291456]{0:T(1024)(128)(4,1)}), s8[2097152]{0:T(1024)(128)(4,1)S(1)}, s32[]{:S(2)}) async-start(s8[6291456]{0:T(1024)(128)(4,1)} %bitcast.17), calls=%async_computation.9 | async-start | bytes 4194304
  313.5 8.7 %slice-start.7 = ((s8[6291456]{0:T(1024)(128)(4,1)}), s8[2097152]{0:T(1024)(128)(4,1)S(1)}, s32[]{:S(2)}) async-start(s8[6291456]{0:T(1024)(128)(4,1)} %bitcast.15), calls=%async_computation.7 | async-start | bytes 4194304
  319.1 6.4 %slice-start.4 = ((s8[6291456]{0:T(1024)(128)(4,1)}), s8[4194304]{0:T(1024)(128)(4,1)S(1)}, s32[]{:S(2)}) async-start(s8[6291456]{0:T(1024)(128)(4,1)} %bitcast.13), calls=%async_computation.4 | async-start | bytes 8388608
  319.1 11.9 %slice-start.2 = ((s8[6291456]{0:T(1024)(128)(4,1)}), s8[4194304]{0:T(1024)(128)(4,1)S(1)}, s32[]{:S(2)}) async-start(s8[6291456]{0:T(1024)(128)(4,1)} %bitcast.11), calls=%async_computation.2 | async-start | bytes 8388608
  322.3 5.5 %slice-start.5 = ((s8[6291456]{0:T(1024)(128)(4,1)}), s8[2097152]{0:T(1024)(128)(4,1)S(1)}, s32[]{:S(2)}) async-start(s8[6291456]{0:T(1024)(128)(4,1)} %bitcast.13), calls=%async_computation.5 | async-start | bytes 4194304
  322.3 8.7 %slice-start.3 = ((s8[6291456]{0:T(1024)(128)(4,1)}), s8[2097152]{0:T(1024)(128)(4,1)S(1)}, s32[]{:S(2)}) async-start(s8[6291456]{0:T(1024)(128)(4,1)} %bitcast.11), calls=%async_computation.3 | async-start | bytes 4194304
  327.8 6.4 %slice-start = ((s8[6291456]{0:T(1024)(128)(4,1)}), s8[4194304]{0:T(1024)(128)(4,1)S(1)}, s32[]{:S(2)}) async-start(s8[6291456]{0:T(1024)(128)(4,1)} %bitcast.9), calls=%async_computation | async-start | bytes 8388608
  331.0 4.2 %slice-start.1 = ((s8[6291456]{0:T(1024)(128)(4,1)}), s8[2097152]{0:T(1024)(128)(4,1)S(1)}, s32[]{:S(2)}) async-start(s8[6291456]{0:T(1024)(128)(4,1)} %bitcast.9), calls=%async_computation.1 | async-start | bytes 4194304

commit v2 on v1

--- a/solution.py
+++ b/solution.py
@@ -185,6 +185,8 @@
             self.ag_first(mat, level - 1)
         else:
             self.ag_last(mat, 0)
+            for level in range(AXES):
+                self.bulk(mat, level, None, True)
 
     def norm_copy(self, stage, delta):
         tor = self.tor
@@ -217,11 +219,6 @@
             self.norm_buf[4, 4] = total
 
     def drain(self):
-        def one(mat, carry):
-            for level in range(AXES):
-                self.bulk(mat, level, None, True)
-            return carry
-        lax.fori_loop(0, NMAT, one, 0)
         for stage in range(4):
             for delta in (self.deltas(stage)):
                 self.norm_copy(stage, delta).wait_send()
@@ -233,7 +230,7 @@
             for delta in (1, 2, 3):
                 pl.semaphore_signal(barrier, inc=1, device_id=tor.peer(axis, delta), device_id_type=MESH)
         pl.semaphore_signal(barrier, inc=1, device_id={'data': 1 - tor.core}, device_id_type=MESH)
-        pl.semaphore_wait(barrier, 10)
+        return barrier
 
 
 SUB = 64
@@ -245,20 +242,21 @@
 ROWS_ROWS = (((0,), (0,)), ((), ()))
 COLS_COLS = (((1,), (1,)), ((), ()))
 COMPUTE_SLOTS = 40
+FIRST_SWAP = 2
 STEP_SLOTS = (
-    (7, 11, 15, 17, 18, 22, 24, 25, 26, 31, 33, 46, 50),
-    (17, 20, 24, 28, 40, 41, 43, 44, 45, 47, 50, 58, 64),
-    (27, 31, 41, 42, 43, 44, 45, 46, 49, 55, 62, 72, 79),
-    (39, 40, 41, 42, 43, 44, 45, 47, 60, 66, 76, 85, 92),
+    (9, 14, 20, 25, 28, 37, 41, 43, 46, 48, 49, 51, 55),
+    (18, 21, 27, 30, 36, 40, 43, 45, 48, 51, 54, 58, 66),
+    (28, 33, 37, 42, 44, 47, 48, 50, 52, 56, 61, 71, 80),
+    (39, 41, 43, 46, 48, 49, 51, 55, 61, 75, 81, 90, 98),
 )
-NORM_SLOTS = (45, 46, 47, 48, 50)
-ADAM_RUNS = ((50, 48, 0),)
-ADAM_READY = 42
+NORM_SLOTS = (52, 53, 54, 55, 56)
+ADAM_RUNS = ((56, 48, 0),)
+ADAM_READY = 44
 LANES = 12
 AHEAD = 8
 PER_SLOT = 2
 PIECES = 24
-SLOTS = 98
+SLOTS = 104
 GELU_A = 0.7978845608028654
 GELU_B = 0.044715
 
@@ -271,6 +269,9 @@
 
 N_ACTS = 11
 N_STATE = 3
+N_LATE = 7
+LAST = (NMAT - 1) * PIECES
+SCOPED_BYTES = 67043328 - (NMAT * OWN * D * 4 + 2 * D * FF * 2)
 
 
 def take(refs, count, start=0):
@@ -281,12 +282,13 @@
     x_in, dy_in, w_two, w_three, w_four, h_one, a_one, y_one, h_two, a_two, clip_ref = take(refs, N_ACTS)
     masters, moms, vels = (take(refs, NMAT, N_ACTS + which * NMAT) for which in range(N_STATE))
     outs = refs[N_ACTS + N_STATE * NMAT:]
-    new_w, new_masters, new_moms, new_vels = (take(outs, NMAT, which * NMAT) for which in range(NMAT))
-    norm_ref, x_peer, a_one_peer, a_two_peer = take(outs, NMAT, NMAT * NMAT)
-    (grads, slot_big, slot_mid, slot_low, norm_buf, scale_ref, dh_own, dh_peer, dy_pair, y_pair, a_tile, w_tile, h_tile,
+    mate_w, new_masters, new_vels = (take(outs, NMAT, which * NMAT) for which in range(N_STATE))
+    grads, dh_pair, last_mom, norm_ref, x_peer, a_one_peer, a_two_peer = take(outs, N_LATE, N_STATE * NMAT)
+    (slot_big, slot_mid, slot_low, norm_buf, scale_ref, dy_pair, y_pair, a_tile, w_tile, h_tile,
      rs_send, rs_recv, ag_send, ag_recv, free_sem, slot_sem, nm_send, nm_recv,
      a_tile_sem, w_tile_sem, h_tile_sem, load_sem, dyx_sem, yx_sem, xx_sem, a_one_sem, a_two_sem, dh_sem, dyp_sem,
-     in_sem, out_sem, w_send, w_recv) = outs[NMAT * NMAT + NMAT:]
+     in_sem, out_sem, w_send, w_recv) = outs[N_STATE * NMAT + N_LATE:]
+    dh_own, dh_peer = dh_pair.at[0], dh_pair.at[1]
     tor = Torus()
     ex = Exchange(tor, grads, (slot_big, slot_mid, slot_low), norm_buf, rs_send, rs_recv, ag_send, ag_recv, free_sem, slot_sem, nm_send, nm_recv)
     core = tor.core
@@ -355,18 +357,23 @@
     h_load(1, 0).start()
     a_load(1, 0, 0).start()
     y_load.start()
-    ex.greet()
-    dy_swap.start()
-    for layer in (1, 0):
-        def swap_one(tile, carry, layer=layer):
-            a_swap(layer, tile).start()
-            return carry
-        lax.fori_loop(0, TILES, swap_one, 0)
-        if layer == 1:
-            y_swap.start()
-    x_swap.start()
+    barrier = ex.greet()
     norm_buf[4, 0] = jnp.zeros((OCT, LANE), F32)
     dy_load.wait()
+
+    def first_swaps():
+        pl.semaphore_wait(barrier, 10)
+        dy_swap.start()
+        for layer in (1, 0):
+            def swap_one(tile, carry, layer=layer):
+                a_swap(layer, tile).start()
+                return carry
+            lax.fori_loop(0, TILES, swap_one, 0)
+            if layer == 1:
+                y_swap.start()
+        for tile in range(FIRST_SWAP):
+            dh_swap(1, tile).start()
+        x_swap.start()
 
     def dh_slot(layer, tile):
         slot = lax.rem(tile, BOTH)
@@ -390,7 +397,12 @@
                 dh_own[rows, columns(tile * HALF + half * TILE, TILE)] = (slope * acc.astype(jnp.bfloat16).astype(F32)).astype(jnp.bfloat16)
             return carry
         lax.fori_loop(0, BOTH, part_body, 0)
-        dh_swap(layer, tile).start()
+        if layer == 1:
+            @pl.when(tile >= FIRST_SWAP)
+            def _():
+                dh_swap(layer, tile).start()
+        else:
+            dh_swap(layer, tile).start()
 
     def row_slot(layer, tile):
         slot = lax.rem(tile, BOTH)
@@ -427,14 +439,10 @@
         dh_swap(layer, tile).wait()
         cols = columns(tile * HALF, HALF)
 
-        def part_body(part, carry):
-            mine = columns(part * TILE, TILE)
-            total = lax.dot_general(y_pair[0:D, mine], dh_own[:, cols], ROWS_ROWS, preferred_element_type=F32)
-            total = total + lax.dot_general(y_pair[D:BOTH * D, mine], dh_peer[:, cols], ROWS_ROWS, preferred_element_type=F32)
-            rows = pl.ds(pl.multiple_of(lax.div(tile, 2) * HALF + part * TILE, TILE), TILE)
-            grads[2 * layer, rows, columns(lax.rem(tile, BOTH) * HALF, HALF)] = total
-            return carry
-        lax.fori_loop(0, BOTH, part_body, 0)
+        total = lax.dot_general(y_pair[0:D, :], dh_own[:, cols], ROWS_ROWS, preferred_element_type=F32)
+        total = total + lax.dot_general(y_pair[D:BOTH * D, :], dh_peer[:, cols], ROWS_ROWS, preferred_element_type=F32)
+        rows = pl.ds(pl.multiple_of(lax.div(tile, BOTH) * HALF, HALF), HALF)
+        grads[2 * layer, rows, columns(lax.rem(tile, BOTH) * HALF, HALF)] = total
 
     def dy_slot(tile):
         slot = lax.rem(tile, BOTH)
@@ -452,39 +460,37 @@
             x_swap.wait()
             x_peer_load.start()
         wait_all(w_three_load(tile))
-        acc = lax.dot_general(dh_own[...], w_tile[slot], COLS_COLS, preferred_element_type=F32)
-        dy_pair[0:D, columns(tile * TILE, TILE)] = acc.astype(jnp.bfloat16)
+
+        def part_body(part, carry):
+            rows = pl.ds(pl.multiple_of(part * HALF, HALF), HALF)
+            acc = lax.dot_general(dh_own[rows, :], w_tile[slot], COLS_COLS, preferred_element_type=F32)
+            dy_pair[rows, columns(tile * TILE, TILE)] = acc.astype(jnp.bfloat16)
+            return carry
+        lax.fori_loop(0, BOTH, part_body, 0)
         dyp_swap(tile).start()
 
     def lane_tile(item, which):
         lane = lax.rem(item, LANES)
         return slot_big.at[lax.div(lane, 6), lax.rem(lax.div(lane, 2), 3), which, lax.rem(lane, 2)]
 
-    def w_stage(item):
-        return dh_own.at[piece_rows(lax.rem(item, LANES)), 0:D]
+    def w_stage(mat, piece):
+        part = lax.rem(mat, BOTH) * AXES + lax.div(piece, OCT)
+        return dh_pair.at[lax.div(mat, BOTH), piece_rows(lax.rem(piece, OCT), lax.rem(part, BOTH) * HALF), columns(lax.div(part, BOTH) * D, D)]
 
     def state_view(ref, mat, piece):
         if mat in (1, 3):
             return ref.at[piece_rows(piece), :]
         return ref.at[piece_rows(lax.rem(piece, OCT)), columns(lax.div(piece, OCT) * D, D)]
 
-    def w_view(mat, piece):
-        ref = new_w[mat]
-        if mat in (1, 3):
-            return ref.at[piece_rows(piece, core * OWN), :]
-        return ref.at[piece_rows(lax.rem(piece, OCT), core * HALF), columns(lax.div(piece, OCT) * D, D)]
-
     def state_load(item, which, mat, piece):
         return pltpu.make_async_copy(state_view((moms, vels, masters)[which][mat], mat, piece), lane_tile(item, which), in_sem.at[lax.rem(item, LANES), which])
 
     def state_store(item, which, mat, piece):
-        return pltpu.make_async_copy(lane_tile(item, which), state_view((new_moms, new_vels, new_masters)[which][mat], mat, piece), out_sem.at[lax.rem(item, LANES), which])
-
-    def w_store(item, mat, piece):
-        return pltpu.make_async_copy(w_stage(item), w_view(mat, piece), out_sem.at[lax.rem(item, LANES), N_STATE])
+        target = last_mom if which == 0 else (new_vels, new_masters)[which - 1][mat]
+        return pltpu.make_async_copy(lane_tile(item, which), state_view(target, mat, piece), out_sem.at[lax.rem(item, LANES), which])
 
     def w_swap(item, mat, piece):
-        return pltpu.make_async_remote_copy(src_ref=w_stage(item), dst_ref=w_view(mat, piece), send_sem=w_send.at[lax.rem(item, LANES)], recv_sem=w_recv.at[item], device_id=mate, device_id_type=MESH)
+        return pltpu.make_async_remote_copy(src_ref=w_stage(mat, piece), dst_ref=state_view(mate_w[mat], mat, piece), send_sem=w_send.at[0], recv_sem=w_recv.at[0], device_id=mate, device_id_type=MESH)
 
     def piece_of(item):
         idx = lax.rem(item, PIECES)
@@ -513,10 +519,12 @@
         for_mat(item, body)
 
     def adam_flush(item):
-        for which in range(N_STATE):
+        for which in (1, 2):
             state_store(item, which, 1, 0).wait()
-        w_store(item, 1, 0).wait()
-        w_swap(item, 1, 0).wait_send()
+
+        @pl.when(item >= LAST)
+        def _():
+            state_store(item, 0, 0, 0).wait()
 
     def adam_item(item):
         @pl.when(item >= LANES - AHEAD)
@@ -534,15 +542,20 @@
         mom_new = BETA_ONE * mom[...] + (1.0 - BETA_ONE) * scaled
         vel_new = BETA_TWO * vel[...] + (1.0 - BETA_TWO) * jnp.square(scaled)
         master_new = master[...] - STEP_SIZE * mom_new / (jnp.sqrt(vel_new * VEL_GAIN) + ADAM_EPS)
-        mom[...] = mom_new
         vel[...] = vel_new
         master[...] = master_new
-        w_stage(item)[...] = master_new.astype(jnp.bfloat16)
+
+        mom[...] = mom_new
+        w_stage(mat, piece)[...] = master_new.astype(jnp.bfloat16)
+
+        @pl.when(item < LAST)
+        def _():
+            grads[mat, piece_rows(piece), :] = mom[...]
 
         def body(mat, piece):
             for which in range(N_STATE):
-                state_store(item, which, mat, piece).start()
-            w_store(item, mat, piece).start()
+                if which > 0 or mat == 0:
+                    state_store(item, which, mat, piece).start()
             w_swap(item, mat, piece).start()
         for_mat(item, body)
 
@@ -558,9 +571,9 @@
             body()
 
     def compute(now):
-        during(0, 2, now, lambda: dh_slot(1, now))
-        during(2, 8, now, lambda: row_slot(1, now - 2))
-        during(8, 12, now, lambda: dh_slot(1, now - 6))
+        during(0, 4, now, lambda: dh_slot(1, now))
+        during(4, 10, now, lambda: row_slot(1, now - 4))
+        during(10, 12, now, lambda: dh_slot(1, now - TILES))
         during(12, 18, now, lambda: column_slot(1, now - 12))
         during(18, 22, now, lambda: dy_slot(now - 18))
         during(22, 28, now, lambda: row_slot(0, now - 22))
@@ -598,6 +611,10 @@
             lax.fori_loop(0, PER_SLOT, adam_body, 0)
 
     def slot_body(now, carry):
+        @pl.when(now == FIRST_SWAP)
+        def _():
+            first_swaps()
+
         @pl.when(now < COMPUTE_SLOTS)
         def _():
             compute(now)
@@ -636,11 +653,7 @@
     lax.fori_loop(0, SLOTS, slot_body, 0)
     for item in range(NMAT * PIECES - (LANES - AHEAD), NMAT * PIECES):
         adam_flush(item)
-
-    def w_wait(item, carry):
-        w_swap(item, 1, 0).wait_recv()
-        return carry
-    lax.fori_loop(0, NMAT * PIECES, w_wait, 0)
+    pltpu.make_async_remote_copy(src_ref=dh_pair, dst_ref=dh_pair, send_sem=w_send.at[0], recv_sem=w_recv.at[0], device_id=mate, device_id_type=MESH).wait()
     ex.drain()
 
 
@@ -648,23 +661,22 @@
     bf16 = jnp.bfloat16
     sds = jax.ShapeDtypeStruct
     dma = pltpu.SemaphoreType.DMA
-    whole = [sds((D, FF), bf16), sds((FF, D), bf16)]
     rows = [sds((HALF, FF), F32), sds((OWN, D), F32)]
+    half_w = [sds((HALF, FF), bf16), sds((OWN, D), bf16)]
     in_vmem = pl.BlockSpec(memory_space=pltpu.VMEM)
+    kept = [pltpu.VMEM((NMAT, OWN, D), F32), pltpu.VMEM((BOTH, D, FF), bf16)]
+    swaps = [sds((D, HALF), bf16), sds((D, OWN), bf16), sds((D, OWN), bf16)]
     outs = pl.pallas_call(
         backward_kernel,
-        out_shape=whole * 2 + rows * 6 + [sds((OCT, LANE), F32), sds((D, HALF), bf16), sds((D, OWN), bf16), sds((D, OWN), bf16)],
+        out_shape=half_w * 2 + rows * 4 + kept + [rows[0], sds((OCT, LANE), F32)] + swaps,
         in_specs=[HBM_ANY] * (N_ACTS - 1) + [in_vmem] + [HBM_ANY] * (N_STATE * NMAT),
-        out_specs=[HBM_ANY] * (NMAT * NMAT) + [in_vmem] + [HBM_ANY] * N_STATE,
+        out_specs=[HBM_ANY] * (N_STATE * NMAT) + [in_vmem] * len(kept) + [HBM_ANY, in_vmem] + [HBM_ANY] * len(swaps),
         scratch_shapes=[
-            pltpu.VMEM((NMAT, OWN, D), F32),
             pltpu.VMEM((NSET, AXES, AXES, BOTH) + HALF_SHAPE[0], F32),
             pltpu.VMEM((NSET, AXES, AXES, BOTH) + HALF_SHAPE[1], F32),
             pltpu.VMEM((NSET, AXES, AXES, BOTH) + HALF_SHAPE[2], F32),
             pltpu.VMEM((NMAT + 1, NMAT + 1, OCT, LANE), F32),
             pltpu.VMEM((OCT, LANE), F32),
-            pltpu.VMEM((D, FF), bf16),
-            pltpu.VMEM((D, FF), bf16),
             pltpu.VMEM((BOTH * D, D), bf16),
             pltpu.VMEM((BOTH * D, HALF), bf16),
             pltpu.VMEM((2, BOTH * D, TILE), bf16),
@@ -690,14 +702,117 @@
             dma((2, 6, 2)),
             dma((4, 2)),
             dma((LANES, 3)),
-            dma((LANES, 4)),
-            dma((LANES,)),
-            dma((NMAT * PIECES,)),
+            dma((LANES, N_STATE)),
+            dma((1,)),
+            dma((1,)),
         ],
-        compiler_params=pltpu.CompilerParams(collective_id=0, has_side_effects=True, vmem_limit_bytes=67043328),
+        compiler_params=pltpu.CompilerParams(collective_id=0, has_side_effects=True, vmem_limit_bytes=SCOPED_BYTES),
         name='backward_exchange',
     )(*acts, clip_norm.reshape(1, 1), *masters, *moms, *vels)
-    return outs[:NMAT * NMAT], outs[NMAT * NMAT]
+    return outs[:N_STATE * NMAT], outs[N_STATE * NMAT:N_STATE * NMAT + N_LATE - N_STATE]
+
+
+RING_SLOTS = 8
+READS_AHEAD = 4
+
+
+def finish_kernel(*refs):
+    mate_w, masters, vels = (take(refs, NMAT, which * NMAT) for which in range(N_STATE))
+    moms, own_w, last_mom, norm_in = take(refs, NMAT, N_STATE * NMAT)
+    outs = refs[N_STATE * NMAT + NMAT:]
+    new_w, new_masters, new_moms, new_vels = (take(outs, NMAT, which * NMAT) for which in range(NMAT))
+    norm_out, wide, narrow, wide_in, wide_out, narrow_in, narrow_out, direct_sem = outs[NMAT * NMAT:]
+    norm_out[0, 0] = norm_in[0, 0]
+    core = lax.axis_index('data')
+
+    def block(ref, mat, stream, shift=0):
+        if mat in (1, 3):
+            return ref.at[pl.ds(pl.multiple_of(shift + stream * HALF, HALF), HALF), :]
+        return ref.at[pl.ds(pl.multiple_of(shift, HALF), HALF), pl.ds(stream * D, D)]
+
+    def w_block(mat, stream, side):
+        return block(new_w[mat], mat, stream, side * (OWN if mat in (1, 3) else HALF))
+
+    direct, wides, narrows = [], [], []
+    for mat in range(NMAT):
+        for stream in range(AXES):
+            part = (mat % BOTH) * AXES + stream
+            own = own_w.at[mat // BOTH, pl.ds((part % BOTH) * HALF, HALF), pl.ds((part // BOTH) * D, D)]
+            direct.append((own, w_block(mat, stream, core)))
+            narrows.append((block(mate_w[mat], mat, stream), w_block(mat, stream, 1 - core)))
+            wides.append((block(vels[mat], mat, stream), block(new_vels[mat], mat, stream)))
+            wides.append((block(masters[mat], mat, stream), block(new_masters[mat], mat, stream)))
+            if mat == 0:
+                wides.append((block(last_mom, mat, stream), block(new_moms[mat], mat, stream)))
+            else:
+                direct.append((moms.at[mat, pl.ds(stream * HALF, HALF), :], block(new_moms[mat], mat, stream)))
+
+    def ring(items, buf, in_sem, out_sem):
+        def load(idx):
+            return pltpu.make_async_copy(items[idx][0], buf.at[idx % RING_SLOTS], in_sem.at[idx % RING_SLOTS])
+
+        def store(idx):
+            return pltpu.make_async_copy(buf.at[idx % RING_SLOTS], items[idx][1], out_sem.at[idx % RING_SLOTS])
+
+        def prime():
+            for idx in range(READS_AHEAD):
+                load(idx).start()
+
+        def advance(idx):
+            load(idx).wait()
+            store(idx).start()
+            ahead = idx + READS_AHEAD
+            if ahead < len(items):
+                if ahead >= RING_SLOTS:
+                    store(ahead - RING_SLOTS).wait()
+                load(ahead).start()
+
+        def finish():
+            for idx in range(len(items) - RING_SLOTS, len(items)):
+                store(idx).wait()
+        return prime, advance, finish
+
+    wide_ring = ring(wides, wide, wide_in, wide_out)
+    narrow_ring = ring(narrows, narrow, narrow_in, narrow_out)
+    wide_ring[0]()
+    narrow_ring[0]()
+    straight = [pltpu.make_async_copy(src, dst, direct_sem.at[idx]) for idx, (src, dst) in enumerate(direct)]
+    for idx in range(len(wides)):
+        if idx < len(straight):
+            straight[idx].start()
+        wide_ring[1](idx)
+        if idx < len(narrows):
+            narrow_ring[1](idx)
+    wide_ring[2]()
+    narrow_ring[2]()
+    for copy in straight:
+        copy.wait()
+
+
+def finish(late, kept, last_mom, norm_block):
+    sds = jax.ShapeDtypeStruct
+    bf16 = jnp.bfloat16
+    dma = pltpu.SemaphoreType.DMA
+    rows = [sds((HALF, FF), F32), sds((OWN, D), F32)]
+    in_vmem = pl.BlockSpec(memory_space=pltpu.VMEM)
+    held = [pltpu.with_memory_space_constraint(value, pltpu.VMEM) for value in kept]
+    return pl.pallas_call(
+        finish_kernel,
+        out_shape=[sds((D, FF), bf16), sds((FF, D), bf16)] * 2 + rows * 6 + [sds((1, 1), F32)],
+        in_specs=[HBM_ANY] * (N_STATE * NMAT) + [in_vmem] * BOTH + [HBM_ANY, in_vmem],
+        out_specs=[HBM_ANY] * (NMAT * NMAT) + [pl.BlockSpec(memory_space=pltpu.SMEM)],
+        scratch_shapes=[
+            pltpu.VMEM((RING_SLOTS, HALF, D), F32),
+            pltpu.VMEM((RING_SLOTS, HALF, D), bf16),
+            dma((RING_SLOTS,)),
+            dma((RING_SLOTS,)),
+            dma((RING_SLOTS,)),
+            dma((RING_SLOTS,)),
+            dma((NMAT * OCT,)),
+        ],
+        compiler_params=pltpu.CompilerParams(vmem_limit_bytes=SCOPED_BYTES),
+        name='write_out',
+    )(*late, *held, last_mom, norm_block)
 
 
 def gelu_fn(values):
@@ -722,8 +837,9 @@
     def per_device(act_in, grad_out, w_one, w_two, w_three, w_four, master_one, master_two, master_three, master_four, mom_one, mom_two, mom_three, mom_four, vel_one, vel_two, vel_three, vel_four, clip_norm):
         h_one, a_one, y_one, h_two, a_two = forward(act_in, w_one, w_two, w_three)
         acts = (act_in, grad_out, w_two, w_three, w_four, h_one, a_one, y_one, h_two, a_two)
-        new_state, norm_block = backward(acts, clip_norm, (master_one, master_two, master_three, master_four), (mom_one, mom_two, mom_three, mom_four), (vel_one, vel_two, vel_three, vel_four))
-        return tuple(new_state) + (norm_block[0, 0],)
+        late, (grads, own_w, last_mom, norm_block) = backward(acts, clip_norm, (master_one, master_two, master_three, master_four), (mom_one, mom_two, mom_three, mom_four), (vel_one, vel_two, vel_three, vel_four))
+        *new_state, grad_norm = finish(late, (grads, own_w), last_mom, norm_block)
+        return tuple(new_state) + (grad_norm.reshape(()),)
 
     in_specs = (row_spec, row_spec, full_spec, full_spec, full_spec, full_spec) + (shard_spec,) * 12 + (full_spec,)
     out_specs = (full_spec,) * 4 + (shard_spec,) * 12 + (full_spec,)

time: 338 us -> 325 us (0.962)
  local copies, waits for them, and re-layouts: 73 us -> 0.02 us
  Pallas kernels: 232 us -> 291 us
    unnamed x74 -> x8, local copies, waits for them, and re-layouts: 71.8 us -> 0.02 us
    pallas_call x1 -> x2, Pallas kernels: 232 us -> 291 us  [the longest x1 234 us: backward(): pl.pallas_call(backward_kernel, out_shape=half_w * 2 + rows * 4 + kept +...]
where the time goes in v2:
time: 325 us
  Pallas kernels  291 us (90%)
  matrix products  31.7 us (10%)
    pallas_call x1, Pallas kernels, backward(): pl.pallas_call(backward_kernel, out_shape=half_w * 2 + rows * 4 + kept +...  234 us
    pallas_call x1, Pallas kernels, finish(): pl.pallas_call(finish_kernel, out_shape=[sds((D, FF), bf16), sds((FF, D),...  57.1 us
    dot_general x1, matrix products, forward(): h_one = jnp.dot(act_in, w_one, preferred_element_type=F32).astype(bf16)  13.1 us
    dot_general x1, matrix products, forward(): h_two = jnp.dot(y_one, w_three, preferred_element_type=F32).astype(bf16)  11.7 us
    dot_general x1, matrix products, forward(): y_one = jnp.dot(a_one, w_two, preferred_element_type=F32).astype(bf16)  6.87 us

profile of v2, /device:TPU:1, one launch (start us, length us, event | category | flops | bytes accessed | tf_op | source)
XLA Modules:
  0.0 324.5 jit_solution(7540255918703930791)
XLA Ops:
  1.3 0.0 copy-start
  1.3 13.1 %fusion.5 = (bf16[1024,3072]{1,0:T(8,128)(2,1)S(1)}, bf16[1024,3072]{1,0:T(8,128)(2,1)}) fusion(bf16[1024,1024]{1,0:T(8,128)(2,1)} %refs_0_.1, bf16[1024,3072]{1,0:T(8,128)(2,1)} %param.21), kind=kOutput, calls=%fused_computation.13 | convolution fusion | flops 6477053952 | bytes 20971520 | tf_op jit(solution)/shard_map/dot_general | solution.py:824
  14.4 0.0 copy-start.2
  14.4 0.0 copy-done
  14.4 0.0 copy-start.1
  14.4 6.9 %fusion.13.refs_7_ = bf16[1024,1024]{1,0:T(8,128)(2,1)S(1)} fusion(bf16[1024,3072]{1,0:T(8,128)(2,1)S(1)} %get-tuple-element.83.refs_6_, bf16[3072,1024]{1,0:T(8,128)(2,1)S(1)} %copy-done), kind=kOutput, calls=%fused_computation.23 | convolution fusion | flops 6442450944 | bytes 14680064 | tf_op jit(solution)/shard_map/dot_general | solution.py:826
  21.3 0.0 copy-done.2
  21.3 0.0 copy-done.1
  21.3 0.0 copy-start.3
  21.3 11.7 %fusion.11 = (bf16[1024,3072]{1,0:T(8,128)(2,1)}, bf16[1024,3072]{1,0:T(8,128)(2,1)}) fusion(bf16[1024,1024]{1,0:T(8,128)(2,1)S(1)} %fusion.13.refs_7_, bf16[1024,3072]{1,0:T(8,128)(2,1)S(1)} %copy-done.1), kind=kOutput, calls=%fused_computation.19 | convolution fusion | flops 6477053952 | bytes 20971520 | tf_op jit(solution)/shard_map/dot_general | solution.py:827
  33.0 0.0 copy-done.3
  33.0 234.2 %backward_exchange.1 = (bf16[512,3072]{1,0:T(8,128)(2,1)}, bf16[1536,1024]{1,0:T(8,128)(2,1)}, bf16[512,3072]{1,0:T(8,128)(2,1)}, bf16[1536,1024]{1,0:T(8,128)(2...) custom-call(bf16[1024,1024]{1,0:T(8,128)(2,1)} %refs_0_.1, ...), custom_call_target="tpu_custom_call" | custom-call | tf_op jit(solution)/shard_map/backward_exchange/pallas_call | solution.py:669
  267.2 57.1 %write_out.1 = (bf16[1024,3072]{1,0:T(8,128)(2,1)}, bf16[3072,1024]{1,0:T(8,128)(2,1)}, bf16[1024,3072]{1,0:T(8,128)(2,1)}, bf16[3072,1024]{1,0:T(8,128)(2,1)}, ...) custom-call(bf16[512,3072]{1,0:T(8,128)(2,1)} %get-tuple-element.50., ...), custom_call_target="tpu_custom_call" | custom-call | tf_op jit(solution)/shard_map/write_out/pallas_call | solution.py:799
Async XLA Ops:
  1.3 13.1 %copy-start = (bf16[3072,1024]{1,0:T(8,128)(2,1)S(1)}, bf16[3072,1024]{1,0:T(8,128)(2,1)}, u32[]{:S(2)}) copy-start(bf16[3072,1024]{1,0:T(8,128)(2,1)} %refs_2_.1) | copy-start | bytes 18874372
  14.4 6.9 %copy-start.2 = (bf16[1024,3072]{1,0:T(8,128)(2,1)}, bf16[1024,3072]{1,0:T(8,128)(2,1)S(1)}, u32[]{:S(2)}) copy-start(bf16[1024,3072]{1,0:T(8,128)(2,1)S(1)} %get-tuple-element.83.refs_6_) | copy-start | bytes 18874372
  14.4 6.9 %copy-start.1 = (bf16[1024,3072]{1,0:T(8,128)(2,1)S(1)}, bf16[1024,3072]{1,0:T(8,128)(2,1)}, u32[]{:S(2)}) copy-start(bf16[1024,3072]{1,0:T(8,128)(2,1)} %refs_3_.1) | copy-start | bytes 18874372
  21.3 11.7 %copy-start.3 = (bf16[1024,1024]{1,0:T(8,128)(2,1)}, bf16[1024,1024]{1,0:T(8,128)(2,1)S(1)}, u32[]{:S(2)}) copy-start(bf16[1024,1024]{1,0:T(8,128)(2,1)S(1)} %fusion.13.refs_7_) | copy-start | bytes 6291460

commit v3 on v2

--- a/solution.py
+++ b/solution.py
@@ -20,7 +20,8 @@
 FF = 3072
 HALF = 512
 TILE = 256
-HALF_SHAPE = ((64, 1024), (16, 1024), (8, 512))
+HALF_SHAPE = ((64, D), (16, D), (8, D))
+STEPS = 12
 CHUNK_ROWS = (128, 32, 8)
 AXES = 3
 RING = 4
@@ -68,10 +69,31 @@
     def region(self, mat, stream, level, delta, half):
         rows = CHUNK_ROWS[level]
         row = self.base[stream * AXES + level] + lax.rem(self.pos[(stream + level) % AXES] + delta, RING) * rows
-        if level < BOTH:
-            row = pl.multiple_of(row + half * (rows // BOTH), rows // BOTH)
-            return self.grads.at[mat, pl.ds(row, rows // BOTH), :]
-        return self.grads.at[mat, pl.ds(pl.multiple_of(row, rows), rows), pl.ds(pl.multiple_of(half * HALF, HALF), HALF)]
+        row = pl.multiple_of(row + half * (rows // BOTH), rows // BOTH)
+        return self.grads.at[mat, pl.ds(row, rows // BOTH), :]
+
+    def chunk(self, mat, stream, delta):
+        rows = CHUNK_ROWS[BOTH]
+        row = self.base[stream * AXES + BOTH] + lax.rem(self.pos[(stream + BOTH) % AXES] + delta, RING) * rows
+        return self.grads.at[mat, pl.ds(pl.multiple_of(row, rows), rows), :]
+
+    def ringmate(self, stream, delta):
+        axis = (stream + BOTH) % AXES
+        pos = self.pos[axis]
+        return {'rep': self.tor.rep + (lax.rem(pos + delta, RING) - pos) * RING ** axis, 'data': self.tor.core}
+
+    def far_copy(self, mat, stream, delta, gather):
+        src = self.chunk(mat, stream, 0 if gather else delta)
+        dst = src if gather else self.slots[BOTH].at[lax.rem(mat, NSET), stream, delta - 1]
+        send, recv = (self.ag_send, self.ag_recv) if gather else (self.rs_send, self.rs_recv)
+        return pltpu.make_async_remote_copy(src_ref=src, dst_ref=dst, send_sem=send.at[mat, BOTH], recv_sem=recv.at[mat, BOTH, 0], device_id=self.ringmate(stream, delta), device_id_type=MESH)
+
+    def ringmates(self, body):
+        for stream in range(AXES):
+            def one(delta, carry, stream=stream):
+                body(stream, delta)
+                return carry
+            lax.fori_loop(1, RING, one, 0)
 
     def rs_copy(self, mat, stream, level, msg, side):
         near = 1 + BOTH * side
@@ -95,7 +117,7 @@
         return pltpu.make_async_remote_copy(
             src_ref=ref, dst_ref=ref,
             send_sem=self.ag_send.at[mat, level],
-            recv_sem=self.ag_recv.at[mat, level, msg - msg // BOTH if isinstance(msg, int) else msg],
+            recv_sem=self.ag_recv.at[mat, level, msg],
             device_id=self.neighbour(stream, level, side), device_id_type=MESH)
 
     def pairs(self, body, msgs=1):
@@ -107,7 +129,8 @@
 
     def bulk(self, mat, level, late, gather):
         send, recv = (self.ag_send, self.ag_recv) if gather else (self.rs_send, self.rs_recv)
-        count = AXES * BOTH * (AXES if late is None else 1 + late)
+        kinds = AXES if late is None else 1 if gather else 1 + late
+        count = AXES * AXES if level == BOTH else AXES * BOTH * kinds
         rows = count * HALF_SHAPE[level][0] * HALF_SHAPE[level][1] // D
         ref = self.grads.at[mat, pl.ds(0, rows), :]
         copy = pltpu.make_async_remote_copy(src_ref=ref, dst_ref=ref, send_sem=send.at[mat, level], recv_sem=recv.at[mat, level, late or 0], device_id=self.neighbour(0, level, 0), device_id_type=MESH)
@@ -139,10 +162,6 @@
             ref = self.region(mat, stream, level, 0, half)
             held = self.slots[level]
             total = ref[...] + held[lax.rem(mat, NSET), stream, 2, half] + held[lax.rem(mat, NSET), stream, 1, 1 - half]
-            if level == 2:
-                total = total * (1.0 / 128.0)
-                square = total * total
-                self.norm_buf[4, 0] = self.norm_buf[4, 0] + sum(square[:, col * 128:(col + 1) * 128] for col in range(RING))
             ref[...] = total
         self.pairs(body)
 
@@ -163,28 +182,63 @@
         self.bulk(mat, level, 0, True)
         self.pairs(lambda stream, side, _: self.ag_copy(mat, stream, level, BOTH, side).start())
 
-    def ag_last(self, mat, level):
-        self.bulk(mat, level, 1, True)
+    def far_first(self, mat):
+        @pl.when(mat < NMAT - NSET)
+        def _():
+            pl.semaphore_wait(self.slot_sem.at[mat, BOTH], AXES * AXES)
+        self.ringmates(lambda stream, delta: self.far_copy(mat, stream, delta, False).start())
+
+    def far_last(self, mat):
+        self.bulk(mat, BOTH, 0, False)
+        self.bulk(mat, BOTH, None, False)
+        held = self.slots[BOTH]
+        for stream in range(AXES):
+            ref = self.chunk(mat, stream, 0)
+            total = (ref[...] + held[lax.rem(mat, NSET), stream, 0] + held[lax.rem(mat, NSET), stream, 1] + held[lax.rem(mat, NSET), stream, 2]) * (1.0 / LANE)
+            square = total * total
+            self.norm_buf[4, 0] = self.norm_buf[4, 0] + sum(square[:, col * LANE:(col + 1) * LANE] for col in range(OCT))
+            ref[...] = total
+
+        def tell(stream, delta):
+            peer = self.ringmate(stream, delta)
+            pl.semaphore_signal(self.free_sem.at[mat, BOTH], inc=1, device_id=peer, device_id_type=MESH)
+
+            @pl.when(mat >= NSET)
+            def _():
+                pl.semaphore_signal(self.slot_sem.at[mat - NSET, BOTH], inc=1, device_id=peer, device_id_type=MESH)
+        self.ringmates(tell)
+
+    def far_gather(self, mat):
+        pl.semaphore_wait(self.free_sem.at[mat, BOTH], AXES * AXES)
+        self.ringmates(lambda stream, delta: self.far_copy(mat, stream, delta, True).start())
 
     def step(self, mat, num):
         if num == 0:
             self.rs_first(mat, 0)
-        elif num in (1, 3, 5):
+        elif num in (1, 3):
             self.rs_mid(mat, num // 2)
-        elif num in (2, 4):
-            self.rs_last(mat, num // 2 - 1)
-            self.rs_first(mat, num // 2)
+        elif num == 2:
+            self.rs_last(mat, 0)
+            self.rs_first(mat, 1)
+        elif num == 4:
+            self.rs_last(mat, 1)
+            self.far_first(mat)
+        elif num == 5:
+            self.far_last(mat)
+            self.far_gather(mat)
         elif num == 6:
-            self.rs_last(mat, 2)
-            self.ag_first(mat, 2)
-        elif num in (7, 9, 11):
-            self.ag_mid(mat, 2 - (num - 7) // 2)
-        elif num in (8, 10):
-            level = 2 - (num - 8) // 2
-            self.ag_last(mat, level)
-            self.ag_first(mat, level - 1)
+            self.bulk(mat, BOTH, 0, True)
+            self.ag_first(mat, 1)
+        elif num in (7, 9):
+            self.ag_mid(mat, (9 - num) // 2)
+        elif num == 8:
+            self.bulk(mat, 1, 1, True)
+            self.bulk(mat, 1, BOTH, True)
+            self.ag_first(mat, 0)
+        elif num == 10:
+            self.bulk(mat, 0, 1, True)
         else:
-            self.ag_last(mat, 0)
+            self.bulk(mat, 0, BOTH, True)
             for level in range(AXES):
                 self.bulk(mat, level, None, True)
 
@@ -241,22 +295,22 @@
 HBM_ANY = pl.BlockSpec(memory_space=pl.ANY)
 ROWS_ROWS = (((0,), (0,)), ((), ()))
 COLS_COLS = (((1,), (1,)), ((), ()))
-COMPUTE_SLOTS = 40
+COMPUTE_SLOTS = 7 * TILES + RING
 FIRST_SWAP = 2
 STEP_SLOTS = (
-    (9, 14, 20, 25, 28, 37, 41, 43, 46, 48, 49, 51, 55),
-    (18, 21, 27, 30, 36, 40, 43, 45, 48, 51, 54, 58, 66),
-    (28, 33, 37, 42, 44, 47, 48, 50, 52, 56, 61, 71, 80),
-    (39, 41, 43, 46, 48, 49, 51, 55, 61, 75, 81, 90, 98),
+    (11, 15, 20, 22, 26, 28, 30, 32, 34, 51, 54, 58),
+    (23, 26, 29, 32, 46, 48, 50, 52, 55, 60, 65, 66),
+    (33, 38, 46, 47, 49, 51, 54, 57, 63, 71, 74, 76),
+    (45, 46, 48, 49, 50, 52, 64, 75, 78, 83, 88, 89),
 )
 NORM_SLOTS = (52, 53, 54, 55, 56)
-ADAM_RUNS = ((56, 48, 0),)
-ADAM_READY = 44
+ADAM_RUNS = ((58, 6, 0), (65, 10, 6), (76, 16, 16))
+ADAM_READY = 49
 LANES = 12
 AHEAD = 8
-PER_SLOT = 2
+PER_SLOT = 3
 PIECES = 24
-SLOTS = 104
+SLOTS = 92
 GELU_A = 0.7978845608028654
 GELU_B = 0.044715
 
@@ -371,8 +425,6 @@
             lax.fori_loop(0, TILES, swap_one, 0)
             if layer == 1:
                 y_swap.start()
-        for tile in range(FIRST_SWAP):
-            dh_swap(1, tile).start()
         x_swap.start()
 
     def dh_slot(layer, tile):
@@ -397,35 +449,48 @@
                 dh_own[rows, columns(tile * HALF + half * TILE, TILE)] = (slope * acc.astype(jnp.bfloat16).astype(F32)).astype(jnp.bfloat16)
             return carry
         lax.fori_loop(0, BOTH, part_body, 0)
-        if layer == 1:
-            @pl.when(tile >= FIRST_SWAP)
-            def _():
-                dh_swap(layer, tile).start()
-        else:
-            dh_swap(layer, tile).start()
-
-    def row_slot(layer, tile):
+        dh_swap(layer, tile).start()
+
+    def row_slot(tile):
         slot = lax.rem(tile, BOTH)
 
         @pl.when(tile == 0)
         def _():
-            if layer == 1:
+            for part in range(RING):
+                dyp_swap(part).wait()
+            a_swap(0, tile).wait()
+            a_load(0, tile, 1).start()
+
+        @pl.when(tile < TILES - 1)
+        def _():
+            a_load(0, tile + 1, 0).start()
+            a_swap(0, tile + 1).wait()
+            a_load(0, tile + 1, 1).start()
+        a_load(0, tile, 0).wait()
+        a_load(0, tile, 1).wait()
+        grads[1, pl.ds(pl.multiple_of(tile * TILE, TILE), TILE), :] = lax.dot_general(a_tile[slot], dy_pair[...], ROWS_ROWS, preferred_element_type=F32)
+
+    def half_slot(part, tile):
+        slot = lax.rem(tile, BOTH)
+
+        @pl.when(tile == 0)
+        def _():
+            if part == 1:
                 dy_swap.wait()
                 y_swap.wait_send()
-            else:
-                for part in range(4):
-                    dyp_swap(part).wait()
-            a_swap(layer, tile).wait()
-            a_load(layer, tile, 1).start()
+                a_swap(1, tile).wait()
+                a_load(1, tile, part).start()
 
         @pl.when(tile < TILES - 1)
         def _():
-            a_load(layer, tile + 1, 0).start()
-            a_swap(layer, tile + 1).wait()
-            a_load(layer, tile + 1, 1).start()
-        a_load(layer, tile, 0).wait()
-        a_load(layer, tile, 1).wait()
-        grads[1 + 2 * layer, pl.ds(pl.multiple_of(tile * TILE, TILE), TILE), :] = lax.dot_general(a_tile[slot], dy_pair[...], ROWS_ROWS, preferred_element_type=F32)
+            if part == 1:
+                a_swap(1, tile + 1).wait()
+            a_load(1, tile + 1, part).start()
+        a_load(1, tile, part).wait()
+        rows = pl.ds(pl.multiple_of(tile * TILE, TILE), TILE)
+        mine = slice(part * D, part * D + D)
+        total = lax.dot_general(a_tile[slot, mine, :], dy_pair[mine, :], ROWS_ROWS, preferred_element_type=F32)
+        grads[AXES, rows, :] = total if part == 0 else grads[AXES, rows, :] + total
 
     def column_slot(layer, tile):
         @pl.when(tile == 0)
@@ -494,13 +559,11 @@
 
     def piece_of(item):
         idx = lax.rem(item, PIECES)
-        early = idx < 12
-        rest = idx - 12
-        stream = jnp.where(early, lax.div(lax.rem(idx, 6), BOTH), lax.div(rest, RING))
+        group = lax.div(idx, TILES)
+        stream = lax.div(lax.rem(idx, TILES), BOTH)
         odd = lax.rem(idx, BOTH)
-        far = lax.div(lax.rem(rest + 12, RING), BOTH)
-        delta = jnp.where(idx < 6, 0, jnp.where(early, 3 - BOTH * odd, jnp.where(far == 1, BOTH, 3 - BOTH * odd)))
-        half = jnp.where(early, odd, jnp.where(far == 1, odd, 1 - odd))
+        delta = jnp.where(group == 0, 0, jnp.where(group == AXES, BOTH, AXES - BOTH * odd))
+        half = jnp.where(group == BOTH, 1 - odd, odd)
         pos = jnp.where(stream == 0, ex.pos[0], jnp.where(stream == 1, ex.pos[1], ex.pos[2]))
         return stream * OCT + lax.rem(pos + delta, RING) * BOTH + half
 
@@ -571,14 +634,11 @@
             body()
 
     def compute(now):
-        during(0, 4, now, lambda: dh_slot(1, now))
-        during(4, 10, now, lambda: row_slot(1, now - 4))
-        during(10, 12, now, lambda: dh_slot(1, now - TILES))
-        during(12, 18, now, lambda: column_slot(1, now - 12))
-        during(18, 22, now, lambda: dy_slot(now - 18))
-        during(22, 28, now, lambda: row_slot(0, now - 22))
-        during(28, 34, now, lambda: dh_slot(0, now - 28))
-        during(34, 40, now, lambda: column_slot(0, now - 34))
+        at = 0
+        for count, body in ((TILES, lambda tile: half_slot(0, tile)), (TILES, lambda tile: half_slot(1, tile)), (TILES, lambda tile: dh_slot(1, tile)), (TILES, lambda tile: column_slot(1, tile)),
+                            (RING, dy_slot), (TILES, row_slot), (TILES, lambda tile: dh_slot(0, tile)), (TILES, lambda tile: column_slot(0, tile))):
+            during(at, at + count, now, lambda body=body, at=at: body(now - at))
+            at = at + count
 
     def late(now):
         for stage in range(NMAT + 1):
@@ -634,7 +694,7 @@
 
             @pl.when(num >= 0)
             def _():
-                for want in range(13):
+                for want in range(STEPS):
                     @pl.when(num == want)
                     def _(want=want):
                         ex.step(mat, want)
@@ -674,7 +734,7 @@
         scratch_shapes=[
             pltpu.VMEM((NSET, AXES, AXES, BOTH) + HALF_SHAPE[0], F32),
             pltpu.VMEM((NSET, AXES, AXES, BOTH) + HALF_SHAPE[1], F32),
-            pltpu.VMEM((NSET, AXES, AXES, BOTH) + HALF_SHAPE[2], F32),
+            pltpu.VMEM((NSET, AXES, AXES) + HALF_SHAPE[2], F32),
             pltpu.VMEM((NMAT + 1, NMAT + 1, OCT, LANE), F32),
             pltpu.VMEM((OCT, LANE), F32),
             pltpu.VMEM((BOTH * D, D), bf16),
@@ -685,7 +745,7 @@
             dma((NMAT, AXES)),
             dma((NMAT, AXES, BOTH)),
             dma((NMAT, AXES)),
-            dma((NMAT, AXES, BOTH)),
+            dma((NMAT, AXES, AXES)),
             pltpu.SemaphoreType.REGULAR((NMAT, AXES)),
             pltpu.SemaphoreType.REGULAR((NMAT, AXES)),
             dma((4, 4)),

time: 325 us -> 320 us (0.985)
  Pallas kernels: 291 us -> 286 us
    pallas_call x1, Pallas kernels: 234 us -> 229 us  [backward(): pl.pallas_call(backward_kernel, out_shape=half_w * 2 + rows * 4 + kept +...]
where the time goes in v3:
time: 320 us; the launch traced here: 319 us
  Pallas kernels  286 us (89%)
  matrix products  31.7 us (10%)
    pallas_call x1, Pallas kernels, backward(): pl.pallas_call(backward_kernel, out_shape=half_w * 2 + rows * 4 + kept +...  229 us
    pallas_call x1, Pallas kernels, finish(): pl.pallas_call(finish_kernel, out_shape=[sds((D, FF), bf16), sds((FF, D),...  57.1 us
    dot_general x1, matrix products, forward(): h_one = jnp.dot(act_in, w_one, preferred_element_type=F32).astype(bf16)  13.1 us
    dot_general x1, matrix products, forward(): h_two = jnp.dot(y_one, w_three, preferred_element_type=F32).astype(bf16)  11.7 us
    dot_general x1, matrix products, forward(): y_one = jnp.dot(a_one, w_two, preferred_element_type=F32).astype(bf16)  6.87 us

profile of v3, /device:TPU:1, one launch (start us, length us, event | category | flops | bytes accessed | tf_op | source)
XLA Modules:
  0.0 319.4 jit_solution(4065718184197706784)
XLA Ops:
  1.3 0.0 copy-start
  1.3 13.1 %fusion.5 = (bf16[1024,3072]{1,0:T(8,128)(2,1)S(1)}, bf16[1024,3072]{1,0:T(8,128)(2,1)}) fusion(bf16[1024,1024]{1,0:T(8,128)(2,1)} %refs_0_.1, bf16[1024,3072]{1,0:T(8,128)(2,1)} %param.21), kind=kOutput, calls=%fused_computation.13 | convolution fusion | flops 6477053952 | bytes 20971520 | tf_op jit(solution)/shard_map/dot_general | solution.py:884
  14.4 0.0 copy-start.2
  14.4 0.0 copy-done
  14.4 0.0 copy-start.1
  14.4 6.9 %fusion.13.refs_7_ = bf16[1024,1024]{1,0:T(8,128)(2,1)S(1)} fusion(bf16[1024,3072]{1,0:T(8,128)(2,1)S(1)} %get-tuple-element.83.refs_6_, bf16[3072,1024]{1,0:T(8,128)(2,1)S(1)} %copy-done), kind=kOutput, calls=%fused_computation.23 | convolution fusion | flops 6442450944 | bytes 14680064 | tf_op jit(solution)/shard_map/dot_general | solution.py:886
  21.3 0.0 copy-done.2
  21.3 0.0 copy-done.1
  21.3 0.0 copy-start.3
  21.3 11.7 %fusion.11 = (bf16[1024,3072]{1,0:T(8,128)(2,1)}, bf16[1024,3072]{1,0:T(8,128)(2,1)}) fusion(bf16[1024,1024]{1,0:T(8,128)(2,1)S(1)} %fusion.13.refs_7_, bf16[1024,3072]{1,0:T(8,128)(2,1)S(1)} %copy-done.1), kind=kOutput, calls=%fused_computation.19 | convolution fusion | flops 6477053952 | bytes 20971520 | tf_op jit(solution)/shard_map/dot_general | solution.py:887
  33.0 0.0 copy-done.3
  33.0 229.1 %backward_exchange.1 = (bf16[512,3072]{1,0:T(8,128)(2,1)}, bf16[1536,1024]{1,0:T(8,128)(2,1)}, bf16[512,3072]{1,0:T(8,128)(2,1)}, bf16[1536,1024]{1,0:T(8,128)(2...) custom-call(bf16[1024,1024]{1,0:T(8,128)(2,1)} %refs_0_.1, ...), custom_call_target="tpu_custom_call" | custom-call | tf_op jit(solution)/shard_map/backward_exchange/pallas_call | solution.py:729
  262.1 57.1 %write_out.1 = (bf16[1024,3072]{1,0:T(8,128)(2,1)}, bf16[3072,1024]{1,0:T(8,128)(2,1)}, bf16[1024,3072]{1,0:T(8,128)(2,1)}, bf16[3072,1024]{1,0:T(8,128)(2,1)}, ...) custom-call(bf16[512,3072]{1,0:T(8,128)(2,1)} %get-tuple-element.50., ...), custom_call_target="tpu_custom_call" | custom-call | tf_op jit(solution)/shard_map/write_out/pallas_call | solution.py:859
Async XLA Ops:
  1.3 13.1 %copy-start = (bf16[3072,1024]{1,0:T(8,128)(2,1)S(1)}, bf16[3072,1024]{1,0:T(8,128)(2,1)}, u32[]{:S(2)}) copy-start(bf16[3072,1024]{1,0:T(8,128)(2,1)} %refs_2_.1) | copy-start | bytes 18874372
  14.4 6.9 %copy-start.2 = (bf16[1024,3072]{1,0:T(8,128)(2,1)}, bf16[1024,3072]{1,0:T(8,128)(2,1)S(1)}, u32[]{:S(2)}) copy-start(bf16[1024,3072]{1,0:T(8,128)(2,1)S(1)} %get-tuple-element.83.refs_6_) | copy-start | bytes 18874372
  14.4 6.9 %copy-start.1 = (bf16[1024,3072]{1,0:T(8,128)(2,1)S(1)}, bf16[1024,3072]{1,0:T(8,128)(2,1)}, u32[]{:S(2)}) copy-start(bf16[1024,3072]{1,0:T(8,128)(2,1)} %refs_3_.1) | copy-start | bytes 18874372
  21.3 11.7 %copy-start.3 = (bf16[1024,1024]{1,0:T(8,128)(2,1)}, bf16[1024,1024]{1,0:T(8,128)(2,1)S(1)}, u32[]{:S(2)}) copy-start(bf16[1024,1024]{1,0:T(8,128)(2,1)S(1)} %fusion.13.refs_7_) | copy-start | bytes 6291460
